TPU v7x, 256 devices: a whole 4x4x8 slice. The times are simulated.
256 devices in a mesh: row: 32 (over z_lo, y, core), col: 8 (over x, z_hi).
Axes of the slice: x: 4, y: 4, z: 8 (z_hi: 2, z_lo: 4; z = z_hi * 4 + z_lo), core: 2. Of those that a mesh axis runs over, the one named last changes fastest.
Arguments:
- diag_tile: float32 [1024, 1024], P(('row', 'col')), as said below
- left_row: bfloat16 [1024, 64, 256], P('col', 'row'), may hold values from -0.3984375 to 0.3984375
- right_row: bfloat16 [1024, 64, 256], P('col', 'row'), may hold values from -1.09375 to 1.09375
- right_col: bfloat16 [1024, 32, 256], P('row', 'col'), may hold values from -1.09375 to 1.09375
- bucket_row: int32 [64], P('row'), may hold values from 1 to 4
- bucket_col: int32 [32], P('col'), may hold values from 1 to 4
Outputs:
- panel_row: bfloat16 [1024, 64, 256], P('col', 'row')
- panel_col: bfloat16 [1024, 32, 256], P('row', 'col')
- update_left: bfloat16 [64, 32, 1024, 256], P('row', 'col')
Inputs may be any that keep to these rules, and one draw needn't show every extreme that they name: diag_tile is symmetric positive definite. `bucket_row`: a tile's rank is 64 times its bucket; factor columns from the rank on are not part of the tile. `bucket_col`: as for bucket_row.
All inputs are finite; a program needn't handle non-finite values.
Results may differ from a plain program's by a relative error of at most 0.0062.
Values may be sent and summed in bfloat16 or wider, within the bound.
No kernel may reach another device: no remote copies, remote signals or barrier semaphores. Data moves between devices by JAX's collectives and lax.ppermute only.
A program may use at most 128 MiB of HBM per device.

v0:
```python
import jax
import jax.numpy as jnp
from jax import lax
from jax.sharding import Mesh
from jax.sharding import PartitionSpec as P

RSTEP = 64
ROW_COL = ("row_0", "row_1", "row_2", "col_0", "col_1")
COL = ("col_0", "col_1")
ROW = ("row_0", "row_1", "row_2")


def edges_of(length, count):
    unit = 8 if length >= 8 * count else 1
    return [length // unit * k // count * unit for k in range(1, count)]


def all_blocks(array, axes, turns):
    pieces = array
    for k in turns:
        pieces = lax.all_gather(pieces, axes[k])
    done = turns[::-1]
    back = [done.index(k) for k in range(len(axes))]
    pieces = pieces.transpose(*back, *range(len(axes), pieces.ndim))
    return pieces.reshape(-1, *array.shape)


def joined_along(pieces, dim):
    pieces = jnp.moveaxis(pieces, 0, dim)
    lengths = pieces.shape
    return pieces.reshape(*lengths[:dim], lengths[dim] * lengths[dim + 1], *lengths[dim + 2 :])


def gather_at_once(array, axes, dim):
    cut = max(range(max(1, array.ndim - 1)), key=lambda d: array.shape[d])
    count, gathered = (len(axes), [])
    for first, section in enumerate(jnp.split(array, edges_of(array.shape[cut], count), axis=cut)):
        if section.size:
            turns = [(first - k) % count for k in range(count)]
            gathered.append(all_blocks(section, axes, turns))
    return joined_along(jnp.concatenate(gathered, axis=cut + 1), dim)


def sent_to_all(array, axis):
    copies = jnp.broadcast_to(array, (lax.axis_size(axis), *array.shape))
    return lax.all_to_all(copies, axis, split_axis=0, concat_axis=0, tiled=True)


def gather_directly(array, axis, dim):
    return joined_along(sent_to_all(array, axis), dim)


def mask_columns(right, bucket):
    live = jnp.arange(right.shape[2], dtype=jnp.int32)[None, :] < (RSTEP * bucket)[:, None]
    return jnp.where(live[None, :, :], right, jnp.zeros_like(right))


def solve_whole(inverse, gathered):
    flat = gathered.astype(jnp.float32).reshape(gathered.shape[0], -1)
    solved = jnp.dot(
        inverse, flat, precision=lax.Precision.HIGHEST, preferred_element_type=jnp.float32
    )
    return solved.astype(jnp.bfloat16).reshape(gathered.shape)


def per_device(diag_tile, left_row, right_row, right_col, bucket_row, bucket_col):
    whole_tile = gather_at_once(diag_tile, ROW_COL, 0)
    order = whole_tile.shape[0]
    lower_factor = jnp.linalg.cholesky(whole_tile)
    identity = jnp.eye(order, dtype=jnp.float32)
    inverse = lax.linalg.triangular_solve(lower_factor, identity, left_side=True, lower=True)
    masked_row = mask_columns(right_row, bucket_row)
    masked_col = mask_columns(right_col, bucket_col)
    row_position = lax.axis_index(COL)
    col_position = lax.axis_index(ROW)
    full_row = solve_whole(inverse, gather_directly(masked_row, COL, 0))
    full_col = solve_whole(inverse, lax.all_gather(masked_col, ROW, axis=0, tiled=True))
    panel_row = lax.dynamic_slice_in_dim(
        full_row, row_position * masked_row.shape[0], masked_row.shape[0], 0
    )
    panel_col = lax.dynamic_slice_in_dim(
        full_col, col_position * masked_col.shape[0], masked_col.shape[0], 0
    )
    coupling = jnp.einsum(
        "kia,kjb->ijab", full_row, full_col, preferred_element_type=jnp.float32
    ).astype(jnp.bfloat16)
    update = jnp.einsum(
        "kia,ijab->ijkb",
        gather_directly(left_row, COL, 0),
        coupling,
        preferred_element_type=jnp.float32,
    )
    update_left = (-update).astype(jnp.bfloat16)
    return (panel_row, panel_col, update_left)


def solution(mesh):
    finer = Mesh(mesh.devices.reshape(4, 4, 2, 4, 2), ("row_0", "row_1", "row_2", "col_0", "col_1"))
    return jax.shard_map(
        per_device,
        mesh=finer,
        in_specs=(
            P(ROW_COL, None),
            P(COL, ROW, None),
            P(COL, ROW, None),
            P(ROW, COL, None),
            P(ROW),
            P(COL),
        ),
        out_specs=(P(COL, ROW, None), P(ROW, COL, None), P(ROW, COL, None, None)),
        check_vma=False,
    )
```

profile of v0, /device:TPU:33, one launch (start us, length us, event | category | flops | bytes accessed | tf_op | source)
XLA Modules:
  0.0 668.1 jit_solution(3684466922552582386)
XLA Ops:
  8.1 9.6 %all-gather.20 = f32[4,1,1024]{2,1,0:T(1,128)S(1)} all-gather(f32[1,1,1024]{2,1,0:T(1,128)S(1)} %get-tuple-element.80), channel_id=2, replica_groups=mesh['row_0'=4,'row_1'=4,'row_2'=2,'col_0'=4,'col_1'=2] {'row_1'}, dimensions={0}, use_global_device_ids=true | all-gather | bytes 20480 | tf_op jit(solution)/shard_map/all_gather | solution.py:21
  17.8 11.4 %all-gather.21 = f32[4,4,1024]{2,1,0:T(4,128)S(1)} all-gather(f32[1,4,1024]{2,1,0:T(4,128)S(1)} %copy.51), channel_id=3, replica_groups=mesh['row_0'=4,'row_1'=4,'row_2'=2,'col_0'=4,'col_1'=2] {'row_0'}, dimensions={0}, use_global_device_ids=true | all-gather | bytes 81920 | tf_op jit(solution)/shard_map/all_gather | solution.py:21
  29.2 7.8 %all-gather.2 = f32[8,4,1,1024]{3,1,2,0:T(4,128)S(1)} all-gather(f32[4,4,1,1024]{3,1,2,0:T(4,128)S(1)} %bitcast.207), channel_id=4, replica_groups=mesh['row_0'=4,'row_1'=4,'row_2'=2,'col_0'=4,'col_1'=2] {'col_1'}, dimensions={0}, use_global_device_ids=true | all-gather | bytes 196608 | tf_op jit(solution)/shard_map/all_gather | solution.py:21
  37.0 10.9 %all-gather.3 = f32[8,4,4,1,1024]{4,2,3,1,0:T(4,128)} all-gather(f32[2,4,4,1,1024]{4,2,3,1,0:T(4,128)S(1)} %bitcast.205), channel_id=5, replica_groups=mesh['row_0'=4,'row_1'=4,'row_2'=2,'col_0'=4,'col_1'=2] {'col_0'}, dimensions={0}, use_global_device_ids=true | all-gather | bytes 655360 | tf_op jit(solution)/shard_map/all_gather | solution.py:21
  48.0 9.2 %all-gather.24 = f32[4,1,1024]{2,1,0:T(1,128)S(1)} all-gather(f32[1,1,1024]{2,1,0:T(1,128)S(1)} %get-tuple-element.83), channel_id=12, replica_groups=mesh['row_0'=4,'row_1'=4,'row_2'=2,'col_0'=4,'col_1'=2] {'col_0'}, dimensions={0}, use_global_device_ids=true | all-gather | bytes 20480 | tf_op jit(solution)/shard_map/all_gather | solution.py:21
  57.2 15.2 %all-gather.25 = f32[2,4,1024]{2,1,0:T(4,128)S(1)} all-gather(f32[1,4,1024]{2,1,0:T(4,128)S(1)} %copy.63), channel_id=13, replica_groups=mesh['row_0'=4,'row_1'=4,'row_2'=2,'col_0'=4,'col_1'=2] {'row_2'}, dimensions={0}, use_global_device_ids=true | all-gather | bytes 49152 | tf_op jit(solution)/shard_map/all_gather | solution.py:21
  72.5 9.1 %all-gather.12 = f32[8,4,1,1024]{3,1,2,0:T(4,128)S(1)} all-gather(f32[2,4,1,1024]{3,1,2,0:T(4,128)S(1)} %bitcast.211), channel_id=14, replica_groups=mesh['row_0'=4,'row_1'=4,'row_2'=2,'col_0'=4,'col_1'=2] {'row_1'}, dimensions={0}, use_global_device_ids=true | all-gather | bytes 163840 | tf_op jit(solution)/shard_map/all_gather | solution.py:21
  81.6 13.3 %all-gather.13 = f32[16,2,4,1,1024]{4,2,3,1,0:T(4,128)} all-gather(f32[4,2,4,1,1024]{4,2,3,1,0:T(4,128)S(1)} %bitcast.204), channel_id=15, replica_groups=mesh['row_0'=4,'row_1'=4,'row_2'=2,'col_0'=4,'col_1'=2] {'row_0'}, dimensions={0}, use_global_device_ids=true | all-gather | bytes 655360 | tf_op jit(solution)/shard_map/all_gather | solution.py:21
  95.0 6.8 %all-gather.22 = f32[2,1,1024]{2,1,0:T(1,128)S(1)} all-gather(f32[1,1,1024]{2,1,0:T(1,128)S(1)} %get-tuple-element.81), channel_id=7, replica_groups=mesh['row_0'=4,'row_1'=4,'row_2'=2,'col_0'=4,'col_1'=2] {'row_2'}, dimensions={0}, use_global_device_ids=true | all-gather | bytes 12288 | tf_op jit(solution)/shard_map/all_gather | solution.py:21
  101.8 9.0 %all-gather.23 = f32[4,2,1024]{2,1,0:T(2,128)S(1)} all-gather(f32[1,2,1024]{2,1,0:T(2,128)S(1)} %copy.56), channel_id=8, replica_groups=mesh['row_0'=4,'row_1'=4,'row_2'=2,'col_0'=4,'col_1'=2] {'row_1'}, dimensions={0}, use_global_device_ids=true | all-gather | bytes 40960 | tf_op jit(solution)/shard_map/all_gather | solution.py:21
  110.8 16.5 %all-gather.7 = f32[16,2,1,1024]{3,1,2,0:T(2,128)S(1)} all-gather(f32[4,2,1,1024]{3,1,2,0:T(2,128)S(1)} %bitcast.209), channel_id=9, replica_groups=mesh['row_0'=4,'row_1'=4,'row_2'=2,'col_0'=4,'col_1'=2] {'row_0'}, dimensions={0}, use_global_device_ids=true | all-gather | bytes 163840 | tf_op jit(solution)/shard_map/all_gather | solution.py:21
  127.4 17.1 %all-gather.8 = f32[8,4,2,1,1024]{4,1,3,2,0:T(4,128)} all-gather(f32[4,4,2,1,1024]{4,1,3,2,0:T(4,128)S(1)} %copy.58), channel_id=10, replica_groups=mesh['row_0'=4,'row_1'=4,'row_2'=2,'col_0'=4,'col_1'=2] {'col_1'}, dimensions={0}, use_global_device_ids=true | all-gather | bytes 393216 | tf_op jit(solution)/shard_map/all_gather | solution.py:21
  144.5 7.1 %all-gather.26 = f32[2,1,1024]{2,1,0:T(1,128)S(1)} all-gather(f32[1,1,1024]{2,1,0:T(1,128)S(1)} %get-tuple-element.82), channel_id=17, replica_groups=mesh['row_0'=4,'row_1'=4,'row_2'=2,'col_0'=4,'col_1'=2] {'col_1'}, dimensions={0}, use_global_device_ids=true | all-gather | bytes 12288 | tf_op jit(solution)/shard_map/all_gather | solution.py:21
  151.7 9.0 %all-gather.27 = f32[4,2,1024]{2,1,0:T(2,128)S(1)} all-gather(f32[1,2,1024]{2,1,0:T(2,128)S(1)} %copy.68), channel_id=18, replica_groups=mesh['row_0'=4,'row_1'=4,'row_2'=2,'col_0'=4,'col_1'=2] {'col_0'}, dimensions={0}, use_global_device_ids=true | all-gather | bytes 40960 | tf_op jit(solution)/shard_map/all_gather | solution.py:21
  160.7 16.5 %all-gather.17 = f32[8,2,1,1024]{3,1,2,0:T(2,128)S(1)} all-gather(f32[4,2,1,1024]{3,1,2,0:T(2,128)S(1)} %bitcast.210), channel_id=19, replica_groups=mesh['row_0'=4,'row_1'=4,'row_2'=2,'col_0'=4,'col_1'=2] {'row_2'}, dimensions={0}, use_global_device_ids=true | all-gather | bytes 98304 | tf_op jit(solution)/shard_map/all_gather | solution.py:21
  177.3 10.1 %all-gather.18 = f32[8,4,2,1,1024]{4,1,3,2,0:T(4,128)} all-gather(f32[2,4,2,1,1024]{4,1,3,2,0:T(4,128)S(1)} %copy.70), channel_id=20, replica_groups=mesh['row_0'=4,'row_1'=4,'row_2'=2,'col_0'=4,'col_1'=2] {'row_1'}, dimensions={0}, use_global_device_ids=true | all-gather | bytes 327680 | tf_op jit(solution)/shard_map/all_gather | solution.py:21
  189.1 7.2 %all-to-all-start = ((bf16[8,128,2,256]{3,2,1,0:T(2,128)(2,1)}), bf16[8,128,2,256]{3,2,1,0:T(2,128)(2,1)}, u32[]{:S(2)}, u32[]{:S(2)}) async-start(bf16[8,128,2,256]{3,2,1,0:T(2,128)(2,1)} %broadcast_in_dim.38), calls=%async_computation | async-start | bytes 2097152 | tf_op jit(solution)/shard_map/all_to_all | solution.py:46
  209.0 19.1 %all-gather.42.cloned.1.call-done = f32[16,2,4,2,1,1024]{5,2,4,3,1,0:T(4,128)} async-done(((f32[4,2,4,2,1,1024]{5,2,4,3,1,0:T(4,128)}), f32[16,2,4,2,1,1024]{5,2,4,3,1,0:T(4,128)}) %all-gather.42.cloned.1.call-update) | async-done | bytes 1048592 | tf_op jit(solution)/shard_map/all_gather | solution.py:21
  230.4 5.3 pad_maximum_fusion
  235.7 5.3 reshape.145
  241.0 5.7 copy.73
  246.7 4.5 fusion.1
  253.2 11.7 %cholesky.223 = f32[128,128]{1,0:T(8,128)S(1)} custom-call(f32[128,128]{1,0:T(8,128)S(1)} %cholesky.580), custom_call_target="Cholesky" | custom-call | tf_op jit(solution)/shard_map/jit(cholesky)/cholesky | solution.py:69
  265.0 9.8 %custom-call.62 = f32[1,128,128]{1,2,0:T(8,128)S(1)} custom-call(f32[1,128,128]{2,1,0:T(8,128)S(1)} %get-tuple-element.79), custom_call_target="InvertDiagBlocksLowerTriangular" | custom-call | tf_op jit(solution)/shard_map/jit(cholesky)/cholesky | solution.py:69
  281.2 11.9 %cholesky.244 = f32[128,128]{1,0:T(8,128)S(1)} custom-call(f32[128,128]{1,0:T(8,128)S(1)} %cholesky.584), custom_call_target="Cholesky" | custom-call | tf_op jit(solution)/shard_map/jit(cholesky)/cholesky | solution.py:69
  293.7 9.8 %custom-call.63 = f32[1,128,128]{1,2,0:T(8,128)S(1)} custom-call(f32[1,128,128]{2,1,0:T(8,128)S(1)} %get-tuple-element.76), custom_call_target="InvertDiagBlocksLowerTriangular" | custom-call | tf_op jit(solution)/shard_map/jit(cholesky)/cholesky | solution.py:69
  306.8 11.7 %cholesky.468 = f32[128,128]{1,0:T(8,128)S(1)} custom-call(f32[128,128]{1,0:T(8,128)S(1)} %cholesky.589), custom_call_target="Cholesky" | custom-call | tf_op jit(solution)/shard_map/jit(cholesky)/cholesky | solution.py:69
  319.8 9.8 %custom-call.64 = f32[1,128,128]{1,2,0:T(8,128)S(1)} custom-call(f32[1,128,128]{2,1,0:T(8,128)S(1)} %get-tuple-element.73), custom_call_target="InvertDiagBlocksLowerTriangular" | custom-call | tf_op jit(solution)/shard_map/jit(cholesky)/cholesky | solution.py:69
  333.1 11.9 %cholesky.487 = f32[128,128]{1,0:T(8,128)S(1)} custom-call(f32[128,128]{1,0:T(8,128)S(1)} %cholesky.594), custom_call_target="Cholesky" | custom-call | tf_op jit(solution)/shard_map/jit(cholesky)/cholesky | solution.py:69
  346.3 9.8 %custom-call.65 = f32[1,128,128]{1,2,0:T(8,128)S(1)} custom-call(f32[1,128,128]{2,1,0:T(8,128)S(1)} %get-tuple-element.70), custom_call_target="InvertDiagBlocksLowerTriangular" | custom-call | tf_op jit(solution)/shard_map/jit(cholesky)/cholesky | solution.py:69
  359.5 11.7 %cholesky.506 = f32[128,128]{1,0:T(8,128)S(1)} custom-call(f32[128,128]{1,0:T(8,128)S(1)} %cholesky.599), custom_call_target="Cholesky" | custom-call | tf_op jit(solution)/shard_map/jit(cholesky)/cholesky | solution.py:69
  372.5 10.2 %custom-call.66 = f32[1,128,128]{1,2,0:T(8,128)S(1)} custom-call(f32[1,128,128]{2,1,0:T(8,128)S(1)} %get-tuple-element.67), custom_call_target="InvertDiagBlocksLowerTriangular" | custom-call | tf_op jit(solution)/shard_map/jit(cholesky)/cholesky | solution.py:69
  386.0 11.7 %cholesky.526 = f32[128,128]{1,0:T(8,128)S(1)} custom-call(f32[128,128]{1,0:T(8,128)S(1)} %cholesky.604), custom_call_target="Cholesky" | custom-call | tf_op jit(solution)/shard_map/jit(cholesky)/cholesky | solution.py:69
  399.1 9.8 %custom-call.67 = f32[1,128,128]{1,2,0:T(8,128)S(1)} custom-call(f32[1,128,128]{2,1,0:T(8,128)S(1)} %get-tuple-element.64), custom_call_target="InvertDiagBlocksLowerTriangular" | custom-call | tf_op jit(solution)/shard_map/jit(cholesky)/cholesky | solution.py:69
  411.9 11.9 %cholesky.546 = f32[128,128]{1,0:T(8,128)S(1)} custom-call(f32[128,128]{1,0:T(8,128)S(1)} %cholesky.609), custom_call_target="Cholesky" | custom-call | tf_op jit(solution)/shard_map/jit(cholesky)/cholesky | solution.py:69
  425.1 9.8 %custom-call.68 = f32[1,128,128]{1,2,0:T(8,128)S(1)} custom-call(f32[1,128,128]{2,1,0:T(8,128)S(1)} %get-tuple-element.61), custom_call_target="InvertDiagBlocksLowerTriangular" | custom-call | tf_op jit(solution)/shard_map/jit(cholesky)/cholesky | solution.py:69
  437.5 11.7 %cholesky.564 = f32[128,128]{1,0:T(8,128)S(1)} custom-call(f32[128,128]{1,0:T(8,128)S(1)} %convolution_subtract_fusion.11), custom_call_target="Cholesky" | custom-call | tf_op jit(solution)/shard_map/jit(cholesky)/cholesky | solution.py:69
  456.0 4.9 select_select_fusion
  460.9 27.2 %while.1 = (s32[]{:T(128)}, f32[1024,1024]{1,0:T(8,128)}, s32[8,2]{0,1:T(2,128)S(1)}, f32[8,128,128]{2,1,0:T(8,128)}, s32[]{:T(128)}) while((s32[]{:T(128)}, f32[1024,1024]{1,0:T(8,128)}, s32[8,2]{0,1:T(2,128)S(1)}, f32[8,128,128]{2,1,0:T(8,128)}, s32[]{:T(128)}) %tuple.68), condition=%wide.while_cond, body=%wide.while_body.sunk | while | flops 2 | bytes 132705 | solution.py:71
  488.1 80.2 %custom-call.69 = f32[8,128,128]{1,2,0:T(8,128)} custom-call(f32[8,128,128]{2,1,0:T(8,128)} %get-tuple-element.10), custom_call_target="InvertDiagBlocksLowerTriangular" | custom-call | tf_op jit(solution)/shard_map/triangular_solve | solution.py:71
  589.8 3.5 convolution_subtract_fusion.2
  594.3 11.4 %all-to-all-start.1 = ((bf16[8,128,2,256]{3,1,2,0:T(8,128)(2,1)}), bf16[8,128,2,256]{3,1,2,0:T(8,128)(2,1)}, u32[]{:S(2)}, u32[]{:S(2)}) async-start(bf16[8,128,2,256]{3,1,2,0:T(8,128)(2,1)} %broadcast_in_dim.41), calls=%async_computation.1 | async-start | bytes 2097152 | tf_op jit(solution)/shard_map/all_to_all | solution.py:46
  613.8 4.5 convolution_subtract_fusion.3
  622.1 3.6 convolution_convert_fusion.2
  627.5 9.4 %all-to-all-done.1 = bf16[8,128,2,256]{3,1,2,0:T(8,128)(2,1)} async-done(((bf16[8,128,2,256]{3,1,2,0:T(8,128)(2,1)}), bf16[8,128,2,256]{3,1,2,0:T(8,128)(2,1)}, u32[]{:S(2)}, u32[]{:S(2)}) %all-to-all-start.1) | async-done | bytes 1048608 | tf_op jit(solution)/shard_map/all_to_all | solution.py:46
  641.1 7.4 %convolution_convert_fusion = bf16[1024,1024]{0,1:T(8,128)(2,1)S(1)} fusion(f32[1024,1024]{1,0:T(8,128)S(1)} %copy-done.8, bf16[1024,1024]{1,0:T(8,128)(2,1)S(1)} %bitcast.197), kind=kOutput, calls=%fused_computation.18 | convolution fusion | flops 12885950464 | bytes 8388608 | tf_op jit(solution)/shard_map/dot_general | solution.py:60
  648.5 5.5 fusion
  654.0 6.2 copy.79
  (146 shorter events, 122.8 us)
Async XLA Ops:
  7.2 180.2 %copy-start.10 = (s32[2]{0:T(128)S(1)}, s32[2]{0:T(128)}, u32[]{:S(2)}) copy-start(s32[2]{0:T(128)} %param.10) | copy-start | bytes 28
  7.2 180.3 %copy-start.2 = (bf16[128,2,256]{2,1,0:T(2,128)(2,1)S(1)}, bf16[128,2,256]{2,1,0:T(2,128)(2,1)}, u32[]{:S(2)}) copy-start(bf16[128,2,256]{2,1,0:T(2,128)(2,1)} %param.8) | copy-start | bytes 393220
  7.2 194.0 %all-gather.36.cloned.1.call-start = ((), (), s32[]{:S(2)}) async-start(), calls=%async_computation.3 | async-start | bytes 1572864 | tf_op jit(solution)/shard_map/all_gather | solution.py:21
  29.2 167.3 %copy-start.11 = (s32[4]{0:T(128)S(1)}, s32[4]{0:T(128)}, u32[]{:S(2)}) copy-start(s32[4]{0:T(128)} %param.11) | copy-start | bytes 52
  29.2 167.4 %copy-start.4 = (bf16[32,4,256]{2,1,0:T(4,128)(2,1)S(1)}, bf16[32,4,256]{2,1,0:T(4,128)(2,1)}, u32[]{:S(2)}) copy-start(bf16[32,4,256]{2,1,0:T(4,128)(2,1)} %param.9) | copy-start | bytes 196612
  48.0 155.5 %all-gather.40.cloned.1.call-start = ((), (), s32[]{:S(2)}) async-start(), calls=%async_computation.5 | async-start | bytes 1572864 | tf_op jit(solution)/shard_map/all_gather | solution.py:21
  94.9 111.0 %all-gather.38.cloned.1.call-start = ((), (), s32[]{:S(2)}) async-start(), calls=%async_computation.4 | async-start | bytes 1310720 | tf_op jit(solution)/shard_map/all_gather | solution.py:21
  144.5 83.6 %all-gather.42.cloned.1.call-start = ((), (), s32[]{:S(2)}) async-start(), calls=%async_computation.6 | async-start | bytes 1310720 | tf_op jit(solution)/shard_map/all_gather | solution.py:21
  187.6 13.5 %copy-start.3 = (bf16[128,2,256]{2,1,0:T(2,128)(2,1)S(1)}, bf16[128,2,256]{2,1,0:T(2,128)(2,1)}, u32[]{:S(2)}) copy-start(bf16[128,2,256]{2,1,0:T(2,128)(2,1)} %param.7) | copy-start | bytes 393220
  189.1 404.1 %all-to-all-start = ((bf16[8,128,2,256]{3,2,1,0:T(2,128)(2,1)}), bf16[8,128,2,256]{3,2,1,0:T(2,128)(2,1)}, u32[]{:S(2)}, u32[]{:S(2)}) async-start(bf16[8,128,2,256]{3,2,1,0:T(2,128)(2,1)} %broadcast_in_dim.38), calls=%async_computation | async-start | bytes 2097152 | tf_op jit(solution)/shard_map/all_to_all | solution.py:46
  196.3 442.0 %all-gather.34.cloned.1.call-start = ((), (), s32[]{:S(2)}) async-start(), calls=%async_computation.2 | async-start | bytes 2162688 | tf_op jit(solution)/shard_map/all_gather | solution.py:77
  251.2 2.0 copy-start.1
  568.4 6.4 copy-start
  587.8 2.0 copy-start.5
  594.3 42.6 %all-to-all-start.1 = ((bf16[8,128,2,256]{3,1,2,0:T(8,128)(2,1)}), bf16[8,128,2,256]{3,1,2,0:T(8,128)(2,1)}, u32[]{:S(2)}, u32[]{:S(2)}) async-start(bf16[8,128,2,256]{3,1,2,0:T(8,128)(2,1)} %broadcast_in_dim.41), calls=%async_computation.1 | async-start | bytes 2097152 | tf_op jit(solution)/shard_map/all_to_all | solution.py:46
  608.4 3.2 copy-start.6
  619.9 5.8 copy-start.7
  625.7 1.0 copy-start.9
  638.3 2.8 copy-start.8
Sparse Core Ops, SparseCore 0:
  48.1 24.8 all-gather.35
  95.0 51.5 all-gather.39
  148.5 30.1 all-gather.37
  187.5 40.5 all-gather.41
  230.4 62.9 all-gather.33
where the time goes:
time: 673 us; the launch traced here: 668 us
  other arithmetic  272 us (40%)
  blocking collectives  179 us (27%)
  matrix products  76.4 us (11%)
  local copies, waits for them, and re-layouts  73.7 us (11%)
  waiting for transfers between devices  28.7 us (4%)
  between operations  19.6 us (3%)
  starting transfers between devices  18.9 us (3%)
    all_gather x16, blocking collectives, all_blocks(): pieces = lax.all_gather(pieces, axes[k])  179 us
    another operation x30, other arithmetic, per_device(): lower_factor = jnp.linalg.cholesky(whole_tile)  172 us
    another operation x3, other arithmetic, per_device(): lax.linalg.triangular_solve(lower_factor, identity, left_side=True, lower...  85.1 us
    another operation x15, matrix products, per_device(): lax.linalg.triangular_solve(lower_factor, identity, left_side=True, lower...  37 us
    another operation x24, local copies, waits for them, and re-layouts  27.2 us
    another operation x14, matrix products, per_device(): lower_factor = jnp.linalg.cholesky(whole_tile)  22.9 us
    all_gather x4, waiting for transfers between devices, all_blocks(): pieces = lax.all_gather(pieces, axes[k])  19.1 us
    unnamed x35, local copies, waits for them, and re-layouts  18.6 us
  transfers between devices with their start and end apart: 7, of which 2 were waited for; matrix products, arithmetic and copies ran while one was open for 59% of the time, Pallas kernels for 0%

commit v1 on v0

v1 whole, which is shorter than its diff:
```python
import functools

import jax
import jax.numpy as jnp
from jax import lax
from jax.experimental import pallas as pl
from jax.experimental.pallas import tpu as pltpu
from jax.sharding import Mesh
from jax.sharding import PartitionSpec as P

RSTEP = 64
F32 = jnp.float32
BF16 = jnp.bfloat16
AXES = ("zl", "y", "c", "x", "zh")
ROW = ("zl", "y", "c")
COL = ("x", "zh")
SENT = 5


def split3(x):
    high = x.astype(BF16)
    rest = x - high.astype(F32)
    middle = rest.astype(BF16)
    low = (rest - middle.astype(F32)).astype(BF16)
    return high, middle, low


def lane_copy(x, lane):
    return jnp.broadcast_to(x[:, lane : lane + 1], (8, 128))


def row_copy(x, row):
    return jnp.broadcast_to(x[row : row + 1, :], (8, 128))


def factor(groups):
    lane = lax.broadcasted_iota(jnp.int32, (8, 128), 1)
    sub = lax.broadcasted_iota(jnp.int32, (8, 128), 0)
    groups = list(groups)
    for j in range(16):
        own = [lane_copy(groups[j], 8 * j + c) for c in range(8)]
        below = {g: [lane_copy(groups[g], 8 * j + c) for c in range(8)] for g in range(j + 1, 16)}
        here = (lane >= 8 * j) & (lane < 8 * j + 8)
        x = jnp.where(here, jnp.where(lane - 8 * j == sub, 1.0, 0.0), groups[j])
        scales, rows, across = [], [], []
        for c in range(8):
            scale = lax.rsqrt(row_copy(own[c], c))
            column = own[c] * scale
            row = row_copy(x, c) * scale
            x = jnp.where(sub == c, row, x) - jnp.where(sub > c, column, 0.0) * row
            lower = {d: row_copy(column, d) for d in range(c + 1, 8)}
            for d in range(c + 1, 8):
                own[d] = own[d] - column * lower[d]
            scales.append(scale)
            rows.append(row)
            across.append(lower)
        groups[j] = x
        for g in range(j + 1, 16):
            cols = below[g]
            w = jnp.where(here, 0.0, groups[g])
            for c in range(8):
                column = cols[c] * scales[c]
                for d in range(c + 1, 8):
                    cols[d] = cols[d] - column * across[c][d]
                w = w - column * rows[c]
            groups[g] = w
    return groups


def dot6(left, right, dims=((1,), (0,))):
    (lh, lm, ll), (rh, rm, rl) = left, right
    dot = functools.partial(lax.dot_general, dimension_numbers=(dims, ((), ())), preferred_element_type=F32)
    lk, rk = dims[0][0], dims[1][0]
    join = lambda a, b, d: jnp.concatenate([a, b], axis=d)
    return (
        dot(join(lh, lm, lk), join(rh, rm, rk))
        + dot(join(lh, lm, lk), join(rm, rh, rk))
        + dot(join(lh, ll, lk), join(rl, rh, rk))
    )


def long_dot6(left, right):
    (lh, lm, ll), (rh, rm, rl) = left, right
    dot = functools.partial(jnp.dot, preferred_element_type=F32)
    return dot(lh, rh) + (dot(lm, rh) + dot(lh, rm)) + (dot(lm, rm) + (dot(ll, rh) + dot(lh, rl)))


def chol_kernel(
    core_ref, mine_ref, other_ref, high_ref, mid_ref, row_ref, low_ref, lh_ref, lm_ref, ll_ref, diag_ref, dh_ref, dm_ref, dl_ref, a_ref
):
    lane = lax.broadcasted_iota(jnp.int32, (128, 128), 1)
    sub = lax.broadcasted_iota(jnp.int32, (128, 128), 0)
    col = lax.broadcasted_iota(jnp.int32, (128, 1024), 1)
    xs_refs = (high_ref, mid_ref, low_ref)
    ls_refs = (lh_ref, lm_ref, ll_ref)
    ds_refs = (dh_ref, dm_ref, dl_ref)
    for ref in (*xs_refs, *ls_refs, *ds_refs, row_ref):
        ref[...] = jnp.zeros_like(ref)
    core = core_ref[0]
    for y in range(4):
        for x in range(4):
            for z in range(4):
                group = z * 2 + y // 2
                for part_ref, half in ((mine_ref, core), (other_ref, 1 - core)):
                    rows = pl.ds(pl.multiple_of(z * 256 + y * 64 + x * 8 + half * 32, 8), 8)
                    for m in range(SENT):
                        block = (group + m) % 8
                        if m == 4 and block < group:
                            continue
                        lanes = slice(128 * m, 128 * m + 128)
                        pieces = [part_ref[4 * y + x, 2 * z + end, :, lanes] for end in range(2)]
                        a_ref[rows, 128 * block : 128 * block + 128] = jnp.concatenate(pieces, axis=0)
    for group in range(5, 8):
        for block in range(group - 4):
            a_ref[128 * block : 128 * block + 128, 128 * group : 128 * group + 128] = jnp.transpose(
                a_ref[128 * group : 128 * group + 128, 128 * block : 128 * block + 128], (1, 0)
            )
    diag_ref[...] = a_ref[0:128, 0:128]

    def settle(at):
        for ref in xs_refs:
            ref[:, pl.ds(at, 128)] = jnp.zeros((1024, 128), BF16)
        row_ref[:, pl.ds(at, 128)] = jnp.where(lane == sub, 1.0, 0.0)
        x = dot6(tuple(ref[...] for ref in ds_refs), split3(row_ref[...]))
        for ref, part in zip(xs_refs, split3(x)):
            ref[pl.ds(at, 128), :] = part
        return x

    def step(k, _):
        at = pl.multiple_of(k * 128, 128)
        before = pl.multiple_of(lax.rem(k + 7, 8) * 128, 128)
        after = pl.multiple_of(lax.rem(k + 1, 8) * 128, 128)
        groups = factor([diag_ref[8 * g : 8 * g + 8, :] for g in range(16)])
        inv = split3(jnp.where(lane <= sub, jnp.concatenate(groups, axis=0), 0.0))
        x = settle(before)
        for ref, part in zip(ls_refs, split3(jnp.transpose(x, (1, 0)))):
            ref[:, pl.ds(before, 128)] = part
        upd = long_dot6(
            tuple(ref[pl.ds(at, 128), :] for ref in ls_refs), tuple(ref[...] for ref in xs_refs)
        )
        row_ref[...] = jnp.where(col >= at, a_ref[pl.ds(at, 128), :], 0.0) - upd
        ahead = a_ref[pl.ds(after, 128), pl.ds(after, 128)] - long_dot6(
            tuple(ref[pl.ds(after, 128), :] for ref in ls_refs),
            tuple(ref[:, pl.ds(after, 128)] for ref in xs_refs),
        )
        side = row_ref[:, pl.ds(after, 128)]
        side_t = split3(jnp.transpose(side, (1, 0)))
        for ref, part in zip(ds_refs, inv):
            ref[...] = part
        x = dot6(inv, split3(side))
        xt = dot6(side_t, inv, ((1,), (1,)))
        diag_ref[...] = ahead - dot6(split3(xt), split3(x))
        return 0

    lax.fori_loop(0, 8, step, 0)
    settle(896)


def chol_inverse(core, mine, other):
    n = 1024
    whole = pl.BlockSpec(memory_space=pltpu.VMEM)
    return pl.pallas_call(
        chol_kernel,
        out_shape=[jax.ShapeDtypeStruct((n, n), BF16)] * 2,
        in_specs=[pl.BlockSpec(memory_space=pltpu.SMEM), whole, whole],
        out_specs=[whole] * 2,
        scratch_shapes=[
            pltpu.VMEM((128, n), F32),
            *[pltpu.VMEM((n, n), BF16)] * 4,
            pltpu.VMEM((128, 128), F32),
            *[pltpu.VMEM((128, 128), BF16)] * 3,
            pltpu.VMEM((n, n), F32),
        ],
        compiler_params=pltpu.CompilerParams(vmem_limit_bytes=40 * 1024 * 1024),
        cost_estimate=pl.CostEstimate(flops=20 * 10**9, bytes_accessed=8 * 2**20, transcendentals=0),
        name="chol_inverse",
    )(core, mine, other)


def panel_kernel(place_ref, row_ref, col_ref, high_ref, mid_ref, near_ref, far_ref, pr_ref, pc_ref, out_ref, p_ref):
    lane = lax.broadcasted_iota(jnp.int32, (256, 256), 1)
    step = pl.program_id(0)

    @pl.when(step == 0)
    def _():
        for i in range(4):
            depth = 256 * (i + 1)
            rows = slice(256 * i, depth)
            high, mid = high_ref[rows, :depth], mid_ref[rows, :depth]
            for t in range(6):
                if t < 2:
                    right = near_ref[: depth // 128, 0, t].reshape(depth, 256)
                    live = RSTEP * row_ref[t]
                else:
                    right = far_ref[: depth // 32, t - 2].reshape(depth, 256)
                    live = RSTEP * col_ref[t - 2]
                solved = jnp.dot(high, right, preferred_element_type=F32)
                solved = solved + jnp.dot(mid, right, preferred_element_type=F32)
                p_ref[t, rows, :] = jnp.where(lane < live, solved, 0.0).astype(BF16)
        for t in range(2):
            pr_ref[t] = p_ref[t, pl.ds(pl.multiple_of(place_ref[0] * 128, 128), 128), :]
        for t in range(4):
            pc_ref[t] = p_ref[2 + t, pl.ds(pl.multiple_of(place_ref[1] * 32, 32), 32), :]

    i, j = step // 4, lax.rem(step, 4)
    coupling = lax.dot_general(p_ref[i], p_ref[2 + j], (((0,), (0,)), ((), ())), preferred_element_type=F32)
    minus = (-coupling).astype(BF16)
    left = near_ref[:, 1, i].reshape(1024, 256)
    out_ref[0, 0] = jnp.dot(left, minus, preferred_element_type=F32).astype(BF16)


def panels(place, bucket_row, bucket_col, high, mid, near, far):
    smem = pl.BlockSpec(memory_space=pltpu.SMEM)
    full = lambda shape: pl.BlockSpec(shape, lambda s: (0,) * len(shape))
    return pl.pallas_call(
        panel_kernel,
        grid=(8,),
        out_shape=[
            jax.ShapeDtypeStruct((2, 128, 256), BF16),
            jax.ShapeDtypeStruct((4, 32, 256), BF16),
            jax.ShapeDtypeStruct((2, 4, 1024, 256), BF16),
        ],
        in_specs=[smem, smem, smem, full(high.shape), full(mid.shape), full(near.shape), full(far.shape)],
        out_specs=[
            full((2, 128, 256)),
            full((4, 32, 256)),
            pl.BlockSpec((1, 1, 1024, 256), lambda s: (s // 4, lax.rem(s, 4), 0, 0)),
        ],
        scratch_shapes=[pltpu.VMEM((6, 1024, 256), BF16)],
        compiler_params=pltpu.CompilerParams(vmem_limit_bytes=40 * 1024 * 1024),
        cost_estimate=pl.CostEstimate(flops=7 * 10**9, bytes_accessed=12 * 2**20, transcendentals=0),
        name="panels",
    )(place, bucket_row, bucket_col, high, mid, near, far)


def sent_to_all(array, axis):
    copies = jnp.broadcast_to(array, (lax.axis_size(axis), *array.shape))
    return lax.all_to_all(copies, axis, split_axis=0, concat_axis=0, tiled=True)


def per_device(diag_tile, left_row, right_row, right_col, bucket_row, bucket_col):
    zl, y, core = (lax.axis_index(axis) for axis in ROW)
    group = 2 * zl + y // 2
    wide = jnp.concatenate([diag_tile, diag_tile[:, :512]], axis=1)
    wide = jnp.concatenate([wide, diag_tile[:, 512:]], axis=1)
    part = lax.dynamic_slice_in_dim(wide, group * 128, SENT * 128, 1)
    part = sent_to_all(part, ("zl", "zh"))
    part = sent_to_all(part, ("y", "x"))
    other = lax.ppermute(part, "c", [(0, 1), (1, 0)])
    near = jnp.stack([right_row, left_row]).transpose(0, 2, 1, 3)
    far = right_col.transpose(1, 0, 2)
    part, other, near, far = lax.optimization_barrier((part, other, near, far))
    near = sent_to_all(near, COL)
    far = sent_to_all(far, ROW)
    high, mid = chol_inverse(core[None], part, other)
    place = jnp.stack([lax.axis_index(COL), lax.axis_index(ROW)])
    panel_row, panel_col, update_left = panels(place, bucket_row, bucket_col, high, mid, near, far)
    return panel_row.transpose(1, 0, 2), panel_col.transpose(1, 0, 2), update_left


def solution(mesh):
    fine = Mesh(mesh.devices.reshape(4, 4, 2, 4, 2), AXES)
    return jax.shard_map(
        per_device,
        mesh=fine,
        in_specs=(
            P(AXES, None),
            P(COL, ROW, None),
            P(COL, ROW, None),
            P(ROW, COL, None),
            P(ROW),
            P(COL),
        ),
        out_specs=(P(COL, ROW, None), P(ROW, COL, None), P(ROW, COL, None, None)),
        check_vma=False,
    )
```

time: 673 us -> 183 us (0.27)
  other arithmetic: 272 us -> 1.17 us
  blocking collectives: 179 us -> 38.5 us
  matrix products: 76.4 us -> 0 us
  local copies, waits for them, and re-layouts: 73.7 us -> 13.2 us
  Pallas kernels: 0 us -> 59.6 us
  waiting for transfers between devices: 28.7 us -> 55.3 us
  between operations: 19.6 us -> 0.78 us
    another operation x33 -> x1, other arithmetic: 257 us -> 0.08 us  [per_device(): place = jnp.stack([lax.axis_index(COL), lax.axis_index(ROW)])]
    all_gather x16 -> x0, blocking collectives: 179 us -> none  [all_blocks(): pieces = lax.all_gather(pieces, axes[k])]
    another operation x29 -> x0, matrix products: 59.9 us -> none  [the longest x15 37 us: per_device(): lax.linalg.triangular_solve(lower_factor, identity, left_side=True, lower...]
    pallas_call x0 -> x2, Pallas kernels: none -> 59.6 us  [the longest x1 46.1 us: chol_inverse(): pl.pallas_call(chol_kernel, out_shape=[jax.ShapeDtypeStruct((n, n), BF16)...]
    all_to_all x2, waiting for transfers between devices: 9.43 us -> 53 us  [sent_to_all(): return lax.all_to_all(copies, axis, split_axis=0, concat_axis=0, tiled=True)]
    all_to_all x0 -> x2, blocking collectives: none -> 38.5 us  [sent_to_all(): return lax.all_to_all(copies, axis, split_axis=0, concat_axis=0, tiled=True)]
    another operation x33 -> x0, local copies, waits for them, and re-layouts: 29.8 us -> none
    all_gather x5 -> x0, waiting for transfers between devices: 19.1 us -> none  [the longest x4 19.1 us: all_blocks(): pieces = lax.all_gather(pieces, axes[k])]
  transfers between devices with their start and end apart: 7 -> 3, of which waited for: 2 -> 2; matrix products, arithmetic and copies ran while one was open for 59% -> 0% of each run, Pallas kernels for 0% -> 25%
where the time goes in v1:
time: 183 us; the launch traced here: 181 us
  Pallas kernels  59.6 us (33%)
  waiting for transfers between devices  55.3 us (30%)
  blocking collectives  38.5 us (21%)
  local copies, waits for them, and re-layouts  13.2 us (7%)
  starting transfers between devices  12.5 us (7%)
    all_to_all x2, waiting for transfers between devices, sent_to_all(): return lax.all_to_all(copies, axis, split_axis=0, concat_axis=0, tiled=True)  53 us
    pallas_call x1, Pallas kernels, chol_inverse(): pl.pallas_call(chol_kernel, out_shape=[jax.ShapeDtypeStruct((n, n), BF16)...  46.1 us
    all_to_all x2, blocking collectives, sent_to_all(): return lax.all_to_all(copies, axis, split_axis=0, concat_axis=0, tiled=True)  38.5 us
    pallas_call x1, Pallas kernels, panels(): pl.pallas_call(panel_kernel, grid=(8,), out_shape=[jax.ShapeDtypeStruct((...  13.6 us
    unnamed x24, local copies, waits for them, and re-layouts  9.75 us
    all_to_all x2, starting transfers between devices, sent_to_all(): return lax.all_to_all(copies, axis, split_axis=0, concat_axis=0, tiled=True)  9 us
  transfers between devices with their start and end apart: 3, of which 2 were waited for; matrix products, arithmetic and copies ran while one was open for 0% of the time, Pallas kernels for 25%

profile of v1, /device:TPU:33, one launch (start us, length us, event | category | flops | bytes accessed | tf_op | source)
XLA Modules:
  0.0 181.1 jit_solution(10877687900114401727)
XLA Ops:
  0.7 0.7 fusion
  1.4 0.0 copy-start.8
  1.4 0.0 copy-start.9
  1.4 14.1 %all_to_all.20 = f32[8,4,640]{2,1,0:T(4,128)S(1)} all-to-all(f32[8,4,640]{2,1,0:T(4,128)S(1)} %broadcast_in_dim.16), channel_id=1, replica_groups=mesh['zl'=4,'y'=4,'c'=2,'x'=4,'zh'=2] {'zl','zh'}, dimensions={0} | all-to-all | bytes 163840 | tf_op jit(solution)/shard_map/all_to_all | solution.py:238
  15.5 0.2 broadcast_in_dim.17
  15.7 24.5 %all_to_all.21.mine_ref = f32[16,8,4,640]{3,2,1,0:T(4,128)S(1)} all-to-all(f32[16,8,4,640]{3,2,1,0:T(4,128)S(1)} %broadcast_in_dim.17), channel_id=1, replica_groups=mesh['zl'=4,'y'=4,'c'=2,'x'=4,'zh'=2] {'y','x'}, dimensions={0} | all-to-all | bytes 2621440 | tf_op jit(solution)/shard_map/all_to_all | solution.py:238
  40.2 3.5 %collective-permute-start = (f32[16,8,4,640]{3,2,1,0:T(4,128)S(1)}, f32[16,8,4,640]{3,2,1,0:T(4,128)S(1)}, u32[]{:S(2)}, u32[]{:S(2)}) collective-permute-start(f32[16,8,4,640]{3,2,1,0:T(4,128)S(1)} %all_to_all.21.mine_ref), channel_id=1, source_target_pairs={{0,8},{8,0},{1,9},{9,1},{2,10},{10,2},{3,11},{11,3},{4,12},{12,4},... | collective-permute-start | bytes 3932168 | tf_op jit(solution)/shard_map/ppermute | solution.py:249
  43.7 0.0 copy-done.8
  43.7 0.0 copy-done.9
  43.7 0.4 maximum_bitcast_fusion
  44.1 2.3 %collective-permute-done.other_ref = f32[16,8,4,640]{3,2,1,0:T(4,128)S(1)} collective-permute-done((f32[16,8,4,640]{3,2,1,0:T(4,128)S(1)}, f32[16,8,4,640]{3,2,1,0:T(4,128)S(1)}, u32[]{:S(2)}, u32[]{:S(2)}) %collective-permute-start) | collective-permute-done | bytes 1310752 | tf_op jit(solution)/shard_map/ppermute | solution.py:249
  46.3 0.0 copy-start
  46.3 1.1 copy-done
  47.5 1.6 broadcast_in_dim.18
  49.0 0.0 copy-start.10
  49.0 3.7 %all-to-all-start.2 = ((bf16[8,2,2,128,256]{4,3,2,1,0:T(8,128)(2,1)}), bf16[8,2,2,128,256]{4,3,2,1,0:T(8,128)(2,1)S(1)}, u32[]{:S(2)}, u32[]{:S(2)}) async-start(bf16[8,2,2,128,256]{4,3,2,1,0:T(8,128)(2,1)} %broadcast_in_dim.18), calls=%async_computation.2 | async-start | bytes 4194304 | tf_op jit(solution)/shard_map/all_to_all | solution.py:238
  52.8 0.0 copy-done.10
  52.8 53.0 %all-to-all-done.2.near_ref = bf16[8,2,2,128,256]{4,3,2,1,0:T(8,128)(2,1)S(1)} async-done(((bf16[8,2,2,128,256]{4,3,2,1,0:T(8,128)(2,1)}), bf16[8,2,2,128,256]{4,3,2,1,0:T(8,128)(2,1)S(1)}, u32[]{:S(2)}, u32[]{:S(2)}) %all-to-all-start.2) | async-done | bytes 2097184 | tf_op jit(solution)/shard_map/all_to_all | solution.py:238
  105.8 1.6 broadcast_in_dim.19
  107.4 5.3 %all-to-all-start.3 = ((bf16[32,4,32,256]{3,2,1,0:T(8,128)(2,1)}), bf16[32,4,32,256]{3,2,1,0:T(8,128)(2,1)}, u32[]{:S(2)}, u32[]{:S(2)}) async-start(bf16[32,4,32,256]{3,2,1,0:T(8,128)(2,1)} %broadcast_in_dim.19), calls=%async_computation.3 | async-start | bytes 4194304 | tf_op jit(solution)/shard_map/all_to_all | solution.py:238
  112.7 0.1 pad_add_fusion.place_ref
  112.8 0.0 copy-start.1
  112.8 1.3 copy-done.1
  114.1 0.0 copy-start.2
  114.1 0.0 copy-start.3
  114.1 46.1 %chol_inverse.1 = (bf16[1024,1024]{1,0:T(8,128)(2,1)S(1)}, bf16[1024,1024]{1,0:T(8,128)(2,1)S(1)}) custom-call(s32[1]{0:T(128)} %bitcast.2.core_ref, f32[16,8,4,640]{3,2,1,0:T(4,128)S(1)} %all_to_all.21.mine_ref, f32[16,8,4,640]{3,2,1,0:T(4,128)S(1)} %copy-done.1), custom_call_target="tpu_custom_call" | custom-call | flops 20000000000 | bytes 8388608 | tf_op jit(solution)/shard_map/chol_inverse/pallas_call | solution.py:162
  160.2 0.0 copy-start.4
  160.2 1.3 copy-done.4
  161.5 0.0 copy-start.6
  161.5 1.3 copy-done.6
  162.8 0.0 all-to-all-done.3.far_ref
  162.8 0.0 copy-done.2
  162.8 0.0 copy-done.3
  162.8 0.0 copy-start.5
  162.9 1.6 copy-done.5
  164.4 0.0 copy-start.7
  164.4 1.6 copy-done.7
  166.0 13.6 %panels.1 = (bf16[2,128,256]{2,1,0:T(8,128)(2,1)S(1)}, bf16[4,32,256]{2,1,0:T(8,128)(2,1)S(1)}, bf16[2,4,1024,256]{3,2,1,0:T(8,128)(2,1)}) custom-call(s32[2]{0:T(128)S(1)} %pad_add_fusion.place_ref, s32[2]{0:T(128)S(1)} %copy-done.2, s32[4]{0:T(128)S(1)} %copy-done.3, bf16[1024,1024]{1,0:T(8,128)(2,1)S(1)} %copy-done.5, bf16[1024,1024]{1,0:T(8,128)(2,1)S(1)} %copy-done.7, ...), custom_call_target="tpu_custom_call" | custom-call | flops 7000000000 | bytes 12582912 | tf_op jit(solution)/shard_map/panels/pallas_call | solution.py:215
  179.6 0.8 copy.11
  180.4 0.7 copy.12
  (3 shorter events, 0.1 us)
Async XLA Ops:
  1.4 42.3 %copy-start.8 = (bf16[128,2,256]{2,1,0:T(2,128)(2,1)S(1)}, bf16[128,2,256]{2,1,0:T(2,128)(2,1)}, u32[]{:S(2)}) copy-start(bf16[128,2,256]{2,1,0:T(2,128)(2,1)} %param.7) | copy-start | bytes 393220
  1.4 42.3 %copy-start.9 = (bf16[128,2,256]{2,1,0:T(2,128)(2,1)S(1)}, bf16[128,2,256]{2,1,0:T(2,128)(2,1)}, u32[]{:S(2)}) copy-start(bf16[128,2,256]{2,1,0:T(2,128)(2,1)} %param.8) | copy-start | bytes 393220
  40.2 6.2 %collective-permute-start = (f32[16,8,4,640]{3,2,1,0:T(4,128)S(1)}, f32[16,8,4,640]{3,2,1,0:T(4,128)S(1)}, u32[]{:S(2)}, u32[]{:S(2)}) collective-permute-start(f32[16,8,4,640]{3,2,1,0:T(4,128)S(1)} %all_to_all.21.mine_ref), channel_id=1, source_target_pairs={{0,8},{8,0},{1,9},{9,1},{2,10},{10,2},{3,11},{11,3},{4,12},{12,4},... | collective-permute-start | bytes 3932168 | tf_op jit(solution)/shard_map/ppermute | solution.py:249
  46.3 1.1 copy-start
  49.0 3.7 %copy-start.10 = (bf16[32,4,256]{2,1,0:T(4,128)(2,1)S(1)}, bf16[32,4,256]{2,1,0:T(4,128)(2,1)}, u32[]{:S(2)}) copy-start(bf16[32,4,256]{2,1,0:T(4,128)(2,1)} %param.9) | copy-start | bytes 196612
  49.0 56.8 %all-to-all-start.2 = ((bf16[8,2,2,128,256]{4,3,2,1,0:T(8,128)(2,1)}), bf16[8,2,2,128,256]{4,3,2,1,0:T(8,128)(2,1)S(1)}, u32[]{:S(2)}, u32[]{:S(2)}) async-start(bf16[8,2,2,128,256]{4,3,2,1,0:T(8,128)(2,1)} %broadcast_in_dim.18), calls=%async_computation.2 | async-start | bytes 4194304 | tf_op jit(solution)/shard_map/all_to_all | solution.py:238
  107.4 55.4 %all-to-all-start.3 = ((bf16[32,4,32,256]{3,2,1,0:T(8,128)(2,1)}), bf16[32,4,32,256]{3,2,1,0:T(8,128)(2,1)}, u32[]{:S(2)}, u32[]{:S(2)}) async-start(bf16[32,4,32,256]{3,2,1,0:T(8,128)(2,1)} %broadcast_in_dim.19), calls=%async_computation.3 | async-start | bytes 4194304 | tf_op jit(solution)/shard_map/all_to_all | solution.py:238
  112.8 1.3 copy-start.1
  114.1 48.7 %copy-start.2 = (s32[2]{0:T(128)S(1)}, s32[2]{0:T(128)}, u32[]{:S(2)}) copy-start(s32[2]{0:T(128)} %row_ref.1) | copy-start | bytes 28
  114.1 48.7 %copy-start.3 = (s32[4]{0:T(128)S(1)}, s32[4]{0:T(128)}, u32[]{:S(2)}) copy-start(s32[4]{0:T(128)} %col_ref.1) | copy-start | bytes 52
  160.2 1.3 copy-start.4
  161.5 1.4 copy-start.6
  162.8 1.6 copy-start.5
  164.4 1.6 copy-start.7

commit v2 on v1

--- a/solution.py
+++ b/solution.py
@@ -8,6 +8,7 @@
 from jax.sharding import Mesh
 from jax.sharding import PartitionSpec as P
 
+
 RSTEP = 64
 F32 = jnp.float32
 BF16 = jnp.bfloat16
@@ -37,9 +38,11 @@
     lane = lax.broadcasted_iota(jnp.int32, (8, 128), 1)
     sub = lax.broadcasted_iota(jnp.int32, (8, 128), 0)
     groups = list(groups)
+    spread = lambda g, j: [lane_copy(groups[g], 8 * j + c) for c in range(8)]
+    own = spread(0, 0)
     for j in range(16):
-        own = [lane_copy(groups[j], 8 * j + c) for c in range(8)]
-        below = {g: [lane_copy(groups[g], 8 * j + c) for c in range(8)] for g in range(j + 1, 16)}
+        below = {g: spread(g, j) for g in range(j + 1, 16)}
+        following = spread(j + 1, j + 1) if j < 15 else None
         here = (lane >= 8 * j) & (lane < 8 * j + 8)
         x = jnp.where(here, jnp.where(lane - 8 * j == sub, 1.0, 0.0), groups[j])
         scales, rows, across = [], [], []
@@ -55,15 +58,27 @@
             rows.append(row)
             across.append(lower)
         groups[j] = x
+        solved = [None] * 8
+        for c in range(7, -1, -1):
+            row = rows[c]
+            for d in range(7, c, -1):
+                row = row - across[c][d] * solved[d]
+            solved[c] = row * scales[c]
         for g in range(j + 1, 16):
             cols = below[g]
             w = jnp.where(here, 0.0, groups[g])
             for c in range(8):
+                if g > j + 2:
+                    w = w - cols[c] * solved[c]
+                    continue
                 column = cols[c] * scales[c]
                 for d in range(c + 1, 8):
                     cols[d] = cols[d] - column * across[c][d]
                 w = w - column * rows[c]
+                if g == j + 1:
+                    following = [following[d] - column * row_copy(column, d) for d in range(8)]
             groups[g] = w
+        own = following
     return groups
 
 
@@ -80,21 +95,22 @@
 
 
 def long_dot6(left, right):
-    (lh, lm, ll), (rh, rm, rl) = left, right
+    m = left.shape[0] // 3
     dot = functools.partial(jnp.dot, preferred_element_type=F32)
-    return dot(lh, rh) + (dot(lm, rh) + dot(lh, rm)) + (dot(lm, rm) + (dot(ll, rh) + dot(lh, rl)))
+    a, b, c = dot(left, right[0]), dot(left[: 2 * m], right[1]), dot(left[:m], right[2])
+    return a[:m] + (a[m : 2 * m] + b[:m]) + (b[m:] + (a[2 * m :] + c))
 
 
 def chol_kernel(
-    core_ref, mine_ref, other_ref, high_ref, mid_ref, row_ref, low_ref, lh_ref, lm_ref, ll_ref, diag_ref, dh_ref, dm_ref, dl_ref, a_ref
+    core_ref, mine_ref, other_ref, out_high_ref, out_mid_ref,
+    row_ref, high_ref, mid_ref, low_ref, ls_ref, diag_ref, dh_ref, dm_ref, dl_ref, a_ref, sems,
 ):
     lane = lax.broadcasted_iota(jnp.int32, (128, 128), 1)
     sub = lax.broadcasted_iota(jnp.int32, (128, 128), 0)
     col = lax.broadcasted_iota(jnp.int32, (128, 1024), 1)
     xs_refs = (high_ref, mid_ref, low_ref)
-    ls_refs = (lh_ref, lm_ref, ll_ref)
     ds_refs = (dh_ref, dm_ref, dl_ref)
-    for ref in (*xs_refs, *ls_refs, *ds_refs, row_ref):
+    for ref in (*xs_refs, ls_ref, *ds_refs, row_ref):
         ref[...] = jnp.zeros_like(ref)
     core = core_ref[0]
     for y in range(4):
@@ -126,34 +142,39 @@
             ref[pl.ds(at, 128), :] = part
         return x
 
-    def step(k, _):
+    def step(depth, k, _):
         at = pl.multiple_of(k * 128, 128)
         before = pl.multiple_of(lax.rem(k + 7, 8) * 128, 128)
         after = pl.multiple_of(lax.rem(k + 1, 8) * 128, 128)
         groups = factor([diag_ref[8 * g : 8 * g + 8, :] for g in range(16)])
         inv = split3(jnp.where(lane <= sub, jnp.concatenate(groups, axis=0), 0.0))
         x = settle(before)
-        for ref, part in zip(ls_refs, split3(jnp.transpose(x, (1, 0)))):
-            ref[:, pl.ds(before, 128)] = part
-        upd = long_dot6(
-            tuple(ref[pl.ds(at, 128), :] for ref in ls_refs), tuple(ref[...] for ref in xs_refs)
-        )
+        for n, part in enumerate(split3(jnp.transpose(x, (1, 0)))):
+            for g in range(8):
+                ls_ref[g, 128 * n : 128 * n + 128, pl.ds(before, 128)] = part[128 * g : 128 * g + 128]
+        upd = long_dot6(ls_ref[k, :, :depth], tuple(ref[:depth, :] for ref in xs_refs))
         row_ref[...] = jnp.where(col >= at, a_ref[pl.ds(at, 128), :], 0.0) - upd
         ahead = a_ref[pl.ds(after, 128), pl.ds(after, 128)] - long_dot6(
-            tuple(ref[pl.ds(after, 128), :] for ref in ls_refs),
-            tuple(ref[:, pl.ds(after, 128)] for ref in xs_refs),
+            ls_ref[lax.rem(k + 1, 8), :, :depth], tuple(ref[:depth, pl.ds(after, 128)] for ref in xs_refs)
         )
-        side = row_ref[:, pl.ds(after, 128)]
-        side_t = split3(jnp.transpose(side, (1, 0)))
+        side_t = split3(jnp.transpose(row_ref[:, pl.ds(after, 128)], (1, 0)))
         for ref, part in zip(ds_refs, inv):
             ref[...] = part
-        x = dot6(inv, split3(side))
-        xt = dot6(side_t, inv, ((1,), (1,)))
-        diag_ref[...] = ahead - dot6(split3(xt), split3(x))
+        xt = split3(dot6(side_t, inv, ((1,), (1,))))
+        diag_ref[...] = ahead - dot6(xt, xt, ((1,), (1,)))
         return 0
 
-    lax.fori_loop(0, 8, step, 0)
+    lax.fori_loop(0, 5, functools.partial(step, 512), 0)
+    lax.fori_loop(5, 8, functools.partial(step, 1024), 0)
     settle(896)
+    copies = [
+        pltpu.make_async_copy(high_ref, out_high_ref, sems.at[0]),
+        pltpu.make_async_copy(mid_ref, out_mid_ref, sems.at[1]),
+    ]
+    for copy in copies:
+        copy.start()
+    for copy in copies:
+        copy.wait()
 
 
 def chol_inverse(core, mine, other):
@@ -163,33 +184,46 @@
         chol_kernel,
         out_shape=[jax.ShapeDtypeStruct((n, n), BF16)] * 2,
         in_specs=[pl.BlockSpec(memory_space=pltpu.SMEM), whole, whole],
-        out_specs=[whole] * 2,
+        out_specs=[pl.BlockSpec(memory_space=pl.ANY)] * 2,
         scratch_shapes=[
             pltpu.VMEM((128, n), F32),
-            *[pltpu.VMEM((n, n), BF16)] * 4,
+            *[pltpu.VMEM((n, n), BF16)] * 3,
+            pltpu.VMEM((8, 384, n), BF16),
             pltpu.VMEM((128, 128), F32),
             *[pltpu.VMEM((128, 128), BF16)] * 3,
             pltpu.VMEM((n, n), F32),
+            pltpu.SemaphoreType.DMA((2,)),
         ],
-        compiler_params=pltpu.CompilerParams(vmem_limit_bytes=40 * 1024 * 1024),
+        compiler_params=pltpu.CompilerParams(vmem_limit_bytes=66_000_000),
         cost_estimate=pl.CostEstimate(flops=20 * 10**9, bytes_accessed=8 * 2**20, transcendentals=0),
         name="chol_inverse",
     )(core, mine, other)
 
 
-def panel_kernel(place_ref, row_ref, col_ref, high_ref, mid_ref, near_ref, far_ref, pr_ref, pc_ref, out_ref, p_ref):
+def panel_kernel(
+    place_ref, row_ref, col_ref, high_ref, mid_ref, near0_ref, near1_ref, near2_ref, near3_ref, far_ref,
+    pr_ref, pc_ref, out_ref, p_ref, near_ref,
+):
     lane = lax.broadcasted_iota(jnp.int32, (256, 256), 1)
     step = pl.program_id(0)
 
     @pl.when(step == 0)
     def _():
+        for s, ref in enumerate((near0_ref, near1_ref, near2_ref, near3_ref)):
+            source = lax.rem(place_ref[2] + 4 - s, 4)
+            for q in range(2):
+                end = place_ref[3] if q == 0 else 1 - place_ref[3]
+                rows = pl.ds(pl.multiple_of(source * 256 + end * 128, 128), 128)
+                for kind in range(2):
+                    for t in range(2):
+                        near_ref[2 * kind + t, rows, :] = ref[q, kind, t]
         for i in range(4):
             depth = 256 * (i + 1)
             rows = slice(256 * i, depth)
             high, mid = high_ref[rows, :depth], mid_ref[rows, :depth]
             for t in range(6):
                 if t < 2:
-                    right = near_ref[: depth // 128, 0, t].reshape(depth, 256)
+                    right = near_ref[t, :depth, :]
                     live = RSTEP * row_ref[t]
                 else:
                     right = far_ref[: depth // 32, t - 2].reshape(depth, 256)
@@ -205,13 +239,13 @@
     i, j = step // 4, lax.rem(step, 4)
     coupling = lax.dot_general(p_ref[i], p_ref[2 + j], (((0,), (0,)), ((), ())), preferred_element_type=F32)
     minus = (-coupling).astype(BF16)
-    left = near_ref[:, 1, i].reshape(1024, 256)
-    out_ref[0, 0] = jnp.dot(left, minus, preferred_element_type=F32).astype(BF16)
+    out_ref[0, 0] = jnp.dot(near_ref[2 + i], minus, preferred_element_type=F32).astype(BF16)
 
 
 def panels(place, bucket_row, bucket_col, high, mid, near, far):
     smem = pl.BlockSpec(memory_space=pltpu.SMEM)
     full = lambda shape: pl.BlockSpec(shape, lambda s: (0,) * len(shape))
+    arrays = (high, mid, *near, far)
     return pl.pallas_call(
         panel_kernel,
         grid=(8,),
@@ -220,17 +254,22 @@
             jax.ShapeDtypeStruct((4, 32, 256), BF16),
             jax.ShapeDtypeStruct((2, 4, 1024, 256), BF16),
         ],
-        in_specs=[smem, smem, smem, full(high.shape), full(mid.shape), full(near.shape), full(far.shape)],
+        in_specs=[smem, smem, smem, *[full(array.shape) for array in arrays]],
         out_specs=[
             full((2, 128, 256)),
             full((4, 32, 256)),
             pl.BlockSpec((1, 1, 1024, 256), lambda s: (s // 4, lax.rem(s, 4), 0, 0)),
         ],
-        scratch_shapes=[pltpu.VMEM((6, 1024, 256), BF16)],
-        compiler_params=pltpu.CompilerParams(vmem_limit_bytes=40 * 1024 * 1024),
+        scratch_shapes=[pltpu.VMEM((6, 1024, 256), BF16), pltpu.VMEM((4, 1024, 256), BF16)],
+        compiler_params=pltpu.CompilerParams(vmem_limit_bytes=66_000_000),
         cost_estimate=pl.CostEstimate(flops=7 * 10**9, bytes_accessed=12 * 2**20, transcendentals=0),
         name="panels",
-    )(place, bucket_row, bucket_col, high, mid, near, far)
+    )(place, bucket_row, bucket_col, *arrays)
+
+
+def moved(array, axis, by):
+    count = lax.axis_size(axis)
+    return lax.ppermute(array, axis, [(k, (k + by) % count) for k in range(count)])
 
 
 def sent_to_all(array, axis):
@@ -244,16 +283,18 @@
     wide = jnp.concatenate([diag_tile, diag_tile[:, :512]], axis=1)
     wide = jnp.concatenate([wide, diag_tile[:, 512:]], axis=1)
     part = lax.dynamic_slice_in_dim(wide, group * 128, SENT * 128, 1)
+    near = jnp.stack([right_row, left_row]).transpose(0, 2, 1, 3)
+    swapped = moved(near, "zh", 1)
     part = sent_to_all(part, ("zl", "zh"))
     part = sent_to_all(part, ("y", "x"))
-    other = lax.ppermute(part, "c", [(0, 1), (1, 0)])
-    near = jnp.stack([right_row, left_row]).transpose(0, 2, 1, 3)
+    near = jnp.stack([near, swapped])
+    other = moved(part, "c", 1)
     far = right_col.transpose(1, 0, 2)
     part, other, near, far = lax.optimization_barrier((part, other, near, far))
-    near = sent_to_all(near, COL)
     far = sent_to_all(far, ROW)
+    near = [near, *[moved(near, "x", by) for by in range(1, 4)]]
     high, mid = chol_inverse(core[None], part, other)
-    place = jnp.stack([lax.axis_index(COL), lax.axis_index(ROW)])
+    place = jnp.stack([lax.axis_index(COL), lax.axis_index(ROW), lax.axis_index("x"), lax.axis_index("zh")])
     panel_row, panel_col, update_left = panels(place, bucket_row, bucket_col, high, mid, near, far)
     return panel_row.transpose(1, 0, 2), panel_col.transpose(1, 0, 2), update_left
 

time: 183 us -> 138 us (0.75)
  waiting for transfers between devices: 55.3 us -> 21.5 us
  local copies, waits for them, and re-layouts: 13.2 us -> 7.35 us
  Pallas kernels: 59.6 us -> 56.6 us
    all_to_all x2 -> x1, waiting for transfers between devices: 53 us -> 4.95 us  [sent_to_all(): return lax.all_to_all(copies, axis, split_axis=0, concat_axis=0, tiled=True)]
    ppermute x1 -> x5, waiting for transfers between devices: 2.28 us -> 16.5 us  [moved(): lax.ppermute(array, axis, [(k, (k + by) % count) for k in range(count)])]
    pallas_call x1, Pallas kernels: 46.1 us -> 40.8 us  [chol_inverse(): pl.pallas_call(chol_kernel, out_shape=[jax.ShapeDtypeStruct((n, n), BF16)...]
    all_to_all x2 -> x1, starting transfers between devices: 9 us -> 4.56 us  [sent_to_all(): return lax.all_to_all(copies, axis, split_axis=0, concat_axis=0, tiled=True)]
    unnamed x24 -> x14, local copies, waits for them, and re-layouts: 9.75 us -> 5.47 us
    ppermute x1 -> x5, starting transfers between devices: 3.49 us -> 6.75 us  [moved(): lax.ppermute(array, axis, [(k, (k + by) % count) for k in range(count)])]
    pallas_call x1, Pallas kernels: 13.6 us -> 15.8 us  [panels(): pl.pallas_call(panel_kernel, grid=(8,), out_shape=[jax.ShapeDtypeStruct((...]
  transfers between devices with their start and end apart: 3 -> 6, of which waited for: 2 -> 2; matrix products, arithmetic and copies ran while one was open for 0% -> 1% of each run, Pallas kernels for 25% -> 30%
where the time goes in v2:
time: 138 us
  Pallas kernels  56.6 us (41%)
  blocking collectives  38.6 us (28%)
  waiting for transfers between devices  21.5 us (16%)
  starting transfers between devices  11.3 us (8%)
  local copies, waits for them, and re-layouts  7.35 us (5%)
  other arithmetic  1.47 us (1%)
    pallas_call x1, Pallas kernels, chol_inverse(): pl.pallas_call(chol_kernel, out_shape=[jax.ShapeDtypeStruct((n, n), BF16)...  40.8 us
    all_to_all x2, blocking collectives, sent_to_all(): return lax.all_to_all(copies, axis, split_axis=0, concat_axis=0, tiled=True)  38.6 us
    ppermute x5, waiting for transfers between devices, moved(): lax.ppermute(array, axis, [(k, (k + by) % count) for k in range(count)])  16.5 us
    pallas_call x1, Pallas kernels, panels(): pl.pallas_call(panel_kernel, grid=(8,), out_shape=[jax.ShapeDtypeStruct((...  15.8 us
    ppermute x5, starting transfers between devices, moved(): lax.ppermute(array, axis, [(k, (k + by) % count) for k in range(count)])  6.75 us
    unnamed x14, local copies, waits for them, and re-layouts  5.47 us
    all_to_all x1, waiting for transfers between devices, sent_to_all(): return lax.all_to_all(copies, axis, split_axis=0, concat_axis=0, tiled=True)  4.95 us
    all_to_all x1, starting transfers between devices, sent_to_all(): return lax.all_to_all(copies, axis, split_axis=0, concat_axis=0, tiled=True)  4.56 us
  transfers between devices with their start and end apart: 6, of which 2 were waited for; matrix products, arithmetic and copies ran while one was open for 1% of the time, Pallas kernels for 30%

profile of v2, /device:TPU:33, one launch (start us, length us, event | category | flops | bytes accessed | tf_op | source)
XLA Modules:
  0.0 137.7 jit_solution(2334504371039327870)
XLA Ops:
  0.7 0.7 fusion.2
  1.4 0.0 copy-start.2
  1.4 0.0 copy-start.3
  1.4 14.1 %all_to_all.15 = f32[8,4,640]{2,1,0:T(4,128)S(1)} all-to-all(f32[8,4,640]{2,1,0:T(4,128)S(1)} %broadcast_in_dim.13), channel_id=1, replica_groups=mesh['zl'=4,'y'=4,'c'=2,'x'=4,'zh'=2] {'zl','zh'}, dimensions={0} | all-to-all | bytes 163840 | tf_op jit(solution)/shard_map/all_to_all | solution.py:277
  15.5 0.2 broadcast_in_dim.14
  15.7 0.0 copy-start.4
  15.7 24.6 %all_to_all.16.mine_ref = f32[16,8,4,640]{3,2,1,0:T(4,128)S(1)} all-to-all(f32[16,8,4,640]{3,2,1,0:T(4,128)S(1)} %broadcast_in_dim.14), channel_id=1, replica_groups=mesh['zl'=4,'y'=4,'c'=2,'x'=4,'zh'=2] {'y','x'}, dimensions={0} | all-to-all | bytes 2621440 | tf_op jit(solution)/shard_map/all_to_all | solution.py:277
  40.3 0.0 copy-start
  40.3 1.1 copy-done
  41.4 3.5 %collective-permute-start = (f32[16,8,4,640]{3,2,1,0:T(4,128)S(1)}, f32[16,8,4,640]{3,2,1,0:T(4,128)S(1)}, u32[]{:S(2)}, u32[]{:S(2)}) collective-permute-start(f32[16,8,4,640]{3,2,1,0:T(4,128)S(1)} %all_to_all.16.mine_ref), channel_id=1, source_target_pairs={{0,8},{8,0},{1,9},{9,1},{2,10},{10,2},{3,11},{11,3},{4,12},{12,4},... | collective-permute-start | bytes 3932168 | tf_op jit(solution)/shard_map/ppermute | solution.py:272
  44.9 0.0 copy-done.2
  44.9 0.0 copy-done.3
  45.0 1.3 collective-permute-start.1
  46.2 16.5 %collective-permute-done.1 = bf16[2,2,128,256]{3,2,1,0:T(8,128)(2,1)S(1)} collective-permute-done((bf16[2,2,128,256]{3,2,1,0:T(8,128)(2,1)S(1)}, bf16[2,2,128,256]{3,2,1,0:T(8,128)(2,1)S(1)}, u32[]{:S(2)}, u32[]{:S(2)}) %collective-permute-start.1) | collective-permute-done | bytes 262176 | tf_op jit(solution)/shard_map/ppermute | solution.py:272
  62.7 0.1 pad_maximum_fusion.near0_ref
  62.8 0.0 copy-start.1
  62.8 0.0 collective-permute-done.other_ref
  62.8 0.0 copy-start.5
  62.8 1.2 copy-done.5
  64.0 0.0 copy-done.4
  64.0 1.6 %broadcast_in_dim.15 = bf16[32,4,32,256]{3,2,1,0:T(8,128)(2,1)} broadcast(bf16[4,32,256]{2,1,0:T(8,128)(2,1)S(1)} %copy.11), dimensions={1,2,3} | broadcast | bytes 2162688 | tf_op jit(solution)/shard_map/broadcast_in_dim | solution.py:276
  65.6 4.6 %all-to-all-start.2 = ((bf16[32,4,32,256]{3,2,1,0:T(8,128)(2,1)}), bf16[32,4,32,256]{3,2,1,0:T(8,128)(2,1)}, u32[]{:S(2)}, u32[]{:S(2)}) async-start(bf16[32,4,32,256]{3,2,1,0:T(8,128)(2,1)} %broadcast_in_dim.15), calls=%async_computation.2 | async-start | bytes 4194304 | tf_op jit(solution)/shard_map/all_to_all | solution.py:277
  70.2 0.7 pad_add_fusion.place_ref
  70.8 0.4 collective-permute-start.4
  71.3 1.5 %collective-permute-start.3 = (bf16[2,2,2,128,256]{4,3,2,1,0:T(8,128)(2,1)S(1)}, bf16[2,2,2,128,256]{4,3,2,1,0:T(8,128)(2,1)}, u32[]{:S(2)}, u32[]{:S(2)}) collective-permute-start(bf16[2,2,2,128,256]{4,3,2,1,0:T(8,128)(2,1)S(1)} %pad_maximum_fusion.near0_ref), channel_id=1, source_target_pairs={{0,4},{2,6},{4,0},{6,2},{1,5},{3,7},{5,1},{7,3},{8,12},{10,14},{12... | collective-permute-start | bytes 1572872 | tf_op jit(solution)/shard_map/ppermute | solution.py:272
  72.8 0.0 copy-done.1
  72.8 0.0 collective-permute-start.2
  72.8 40.8 %chol_inverse.1 = (bf16[1024,1024]{1,0:T(8,128)(2,1)}, bf16[1024,1024]{1,0:T(8,128)(2,1)}) custom-call(s32[1]{0:T(128)} %bitcast.4.core_ref, f32[16,8,4,640]{3,2,1,0:T(4,128)} %copy-done, f32[16,8,4,640]{3,2,1,0:T(4,128)} %copy-done.5), custom_call_target="tpu_custom_call" | custom-call | flops 20000000000 | bytes 8388608 | tf_op jit(solution)/shard_map/chol_inverse/pallas_call | solution.py:183
  113.7 0.0 collective-permute-done.4.near3_ref
  113.7 0.0 collective-permute-done.3.near2_ref
  113.7 0.0 collective-permute-done.2.near1_ref
  113.7 5.0 %all-to-all-done.2.far_ref = bf16[32,4,32,256]{3,2,1,0:T(8,128)(2,1)} async-done(((bf16[32,4,32,256]{3,2,1,0:T(8,128)(2,1)}), bf16[32,4,32,256]{3,2,1,0:T(8,128)(2,1)}, u32[]{:S(2)}, u32[]{:S(2)}) %all-to-all-start.2) | async-done | bytes 2097184 | tf_op jit(solution)/shard_map/all_to_all | solution.py:277
  118.6 15.8 %panels.1 = (bf16[2,128,256]{2,1,0:T(8,128)(2,1)}, bf16[4,32,256]{2,1,0:T(8,128)(2,1)}, bf16[2,4,1024,256]{3,2,1,0:T(8,128)(2,1)}) custom-call(s32[4]{0:T(128)} %pad_add_fusion.place_ref, s32[2]{0:T(128)} %row_ref.1, s32[4]{0:T(128)} %col_ref.1, bf16[1024,1024]{1,0:T(8,128)(2,1)} %get-tuple-element.14.high_ref, ...), custom_call_target="tpu_custom_call" | custom-call | flops 7000000000 | bytes 12582912 | tf_op jit(solution)/shard_map/panels/pallas_call | solution.py:249
  134.4 1.7 %copy.12 = bf16[128,2,256]{2,1,0:T(2,128)(2,1)} copy(bf16[128,2,256]{2,0,1:T(8,128)(2,1)} %bitcast.19) | data formatting | bytes 262144
  136.1 1.5 %copy.13 = bf16[32,4,256]{2,1,0:T(4,128)(2,1)} copy(bf16[32,4,256]{2,0,1:T(8,128)(2,1)} %bitcast.21) | data formatting | bytes 131072
  (4 shorter events, 0.1 us)
Async XLA Ops:
  1.4 43.5 %copy-start.2 = (bf16[128,2,256]{2,1,0:T(2,128)(2,1)S(1)}, bf16[128,2,256]{2,1,0:T(2,128)(2,1)}, u32[]{:S(2)}) copy-start(bf16[128,2,256]{2,1,0:T(2,128)(2,1)} %param.7) | copy-start | bytes 393220
  1.4 43.5 %copy-start.3 = (bf16[128,2,256]{2,1,0:T(2,128)(2,1)S(1)}, bf16[128,2,256]{2,1,0:T(2,128)(2,1)}, u32[]{:S(2)}) copy-start(bf16[128,2,256]{2,1,0:T(2,128)(2,1)} %param.8) | copy-start | bytes 393220
  15.7 48.3 %copy-start.4 = (bf16[32,4,256]{2,1,0:T(4,128)(2,1)S(1)}, bf16[32,4,256]{2,1,0:T(4,128)(2,1)}, u32[]{:S(2)}) copy-start(bf16[32,4,256]{2,1,0:T(4,128)(2,1)} %param.9) | copy-start | bytes 196612
  40.3 1.1 copy-start
  41.4 21.4 %collective-permute-start = (f32[16,8,4,640]{3,2,1,0:T(4,128)S(1)}, f32[16,8,4,640]{3,2,1,0:T(4,128)S(1)}, u32[]{:S(2)}, u32[]{:S(2)}) collective-permute-start(f32[16,8,4,640]{3,2,1,0:T(4,128)S(1)} %all_to_all.16.mine_ref), channel_id=1, source_target_pairs={{0,8},{8,0},{1,9},{9,1},{2,10},{10,2},{3,11},{11,3},{4,12},{12,4},... | collective-permute-start | bytes 3932168 | tf_op jit(solution)/shard_map/ppermute | solution.py:272
  45.0 17.8 %collective-permute-start.1 = (bf16[2,2,128,256]{3,2,1,0:T(8,128)(2,1)S(1)}, bf16[2,2,128,256]{3,2,1,0:T(8,128)(2,1)S(1)}, u32[]{:S(2)}, u32[]{:S(2)}) collective-permute-start(bf16[2,2,128,256]{3,2,1,0:T(8,128)(2,1)S(1)} %get-tuple-element.25), channel_id=1, source_target_pairs={{0,1},{1,0},{2,3},{3,2},{4,5},{5,4},{6,7},{7,6},{8,9},{9,8},{10,11... | collective-permute-start | bytes 786440 | tf_op jit(solution)/shard_map/ppermute | solution.py:272
  62.8 10.0 %copy-start.1 = (bf16[2,2,2,128,256]{4,3,2,1,0:T(8,128)(2,1)}, bf16[2,2,2,128,256]{4,3,2,1,0:T(8,128)(2,1)S(1)}, u32[]{:S(2)}) copy-start(bf16[2,2,2,128,256]{4,3,2,1,0:T(8,128)(2,1)S(1)} %pad_maximum_fusion.near0_ref) | copy-start | bytes 1572868
  62.8 1.2 copy-start.5
  65.6 53.0 %all-to-all-start.2 = ((bf16[32,4,32,256]{3,2,1,0:T(8,128)(2,1)}), bf16[32,4,32,256]{3,2,1,0:T(8,128)(2,1)}, u32[]{:S(2)}, u32[]{:S(2)}) async-start(bf16[32,4,32,256]{3,2,1,0:T(8,128)(2,1)} %broadcast_in_dim.15), calls=%async_computation.2 | async-start | bytes 4194304 | tf_op jit(solution)/shard_map/all_to_all | solution.py:277
  70.8 42.8 %collective-permute-start.4 = (bf16[2,2,2,128,256]{4,3,2,1,0:T(8,128)(2,1)S(1)}, bf16[2,2,2,128,256]{4,3,2,1,0:T(8,128)(2,1)}, u32[]{:S(2)}, u32[]{:S(2)}) collective-permute-start(bf16[2,2,2,128,256]{4,3,2,1,0:T(8,128)(2,1)S(1)} %pad_maximum_fusion.near0_ref), channel_id=1, source_target_pairs={{0,6},{2,0},{4,2},{6,4},{1,7},{3,1},{5,3},{7,5},{8,14},{10,8},{12,... | collective-permute-start | bytes 1572872 | tf_op jit(solution)/shard_map/ppermute | solution.py:272
  71.3 42.4 %collective-permute-start.3 = (bf16[2,2,2,128,256]{4,3,2,1,0:T(8,128)(2,1)S(1)}, bf16[2,2,2,128,256]{4,3,2,1,0:T(8,128)(2,1)}, u32[]{:S(2)}, u32[]{:S(2)}) collective-permute-start(bf16[2,2,2,128,256]{4,3,2,1,0:T(8,128)(2,1)S(1)} %pad_maximum_fusion.near0_ref), channel_id=1, source_target_pairs={{0,4},{2,6},{4,0},{6,2},{1,5},{3,7},{5,1},{7,3},{8,12},{10,14},{12... | collective-permute-start | bytes 1572872 | tf_op jit(solution)/shard_map/ppermute | solution.py:272
  72.8 40.9 %collective-permute-start.2 = (bf16[2,2,2,128,256]{4,3,2,1,0:T(8,128)(2,1)S(1)}, bf16[2,2,2,128,256]{4,3,2,1,0:T(8,128)(2,1)}, u32[]{:S(2)}, u32[]{:S(2)}) collective-permute-start(bf16[2,2,2,128,256]{4,3,2,1,0:T(8,128)(2,1)S(1)} %pad_maximum_fusion.near0_ref), channel_id=1, source_target_pairs={{0,2},{2,4},{4,6},{6,0},{1,3},{3,5},{5,7},{7,1},{8,10},{10,12},{12... | collective-permute-start | bytes 1572872 | tf_op jit(solution)/shard_map/ppermute | solution.py:272

commit v3 on v2

--- a/solution.py
+++ b/solution.py
@@ -34,24 +34,28 @@
     return jnp.broadcast_to(x[row : row + 1, :], (8, 128))
 
 
-def factor(groups):
+def factor(groups, first):
     lane = lax.broadcasted_iota(jnp.int32, (8, 128), 1)
     sub = lax.broadcasted_iota(jnp.int32, (8, 128), 0)
-    groups = list(groups)
+    groups = dict(enumerate(groups, first))
+    last = first + 8
     spread = lambda g, j: [lane_copy(groups[g], 8 * j + c) for c in range(8)]
-    own = spread(0, 0)
-    for j in range(16):
-        below = {g: spread(g, j) for g in range(j + 1, 16)}
-        following = spread(j + 1, j + 1) if j < 15 else None
+    own = spread(first, first)
+    for j in range(first, last):
+        below = {g: spread(g, j) for g in range(j + 1, last)}
+        following = spread(j + 1, j + 1) if j + 1 < last else None
         here = (lane >= 8 * j) & (lane < 8 * j + 8)
         x = jnp.where(here, jnp.where(lane - 8 * j == sub, 1.0, 0.0), groups[j])
         scales, rows, across = [], [], []
+        pivot = row_copy(own[0], 0)
         for c in range(8):
-            scale = lax.rsqrt(row_copy(own[c], c))
+            scale = lax.rsqrt(pivot)
             column = own[c] * scale
+            lower = {d: row_copy(own[c], d) * scale for d in range(c + 1, 8)}
+            if c < 7:
+                pivot = row_copy(own[c + 1], c + 1) - lower[c + 1] * lower[c + 1]
             row = row_copy(x, c) * scale
             x = jnp.where(sub == c, row, x) - jnp.where(sub > c, column, 0.0) * row
-            lower = {d: row_copy(column, d) for d in range(c + 1, 8)}
             for d in range(c + 1, 8):
                 own[d] = own[d] - column * lower[d]
             scales.append(scale)
@@ -64,7 +68,7 @@
             for d in range(7, c, -1):
                 row = row - across[c][d] * solved[d]
             solved[c] = row * scales[c]
-        for g in range(j + 1, 16):
+        for g in range(j + 1, last):
             cols = below[g]
             w = jnp.where(here, 0.0, groups[g])
             for c in range(8):
@@ -79,7 +83,7 @@
                     following = [following[d] - column * row_copy(column, d) for d in range(8)]
             groups[g] = w
         own = following
-    return groups
+    return jnp.concatenate([groups[g] for g in range(first, last)], axis=0)
 
 
 def dot6(left, right, dims=((1,), (0,))):
@@ -108,6 +112,8 @@
     lane = lax.broadcasted_iota(jnp.int32, (128, 128), 1)
     sub = lax.broadcasted_iota(jnp.int32, (128, 128), 0)
     col = lax.broadcasted_iota(jnp.int32, (128, 1024), 1)
+    half_lane = lax.broadcasted_iota(jnp.int32, (64, 128), 1)
+    half_sub = lax.broadcasted_iota(jnp.int32, (64, 128), 0)
     xs_refs = (high_ref, mid_ref, low_ref)
     ds_refs = (dh_ref, dm_ref, dl_ref)
     for ref in (*xs_refs, ls_ref, *ds_refs, row_ref):
@@ -146,8 +152,14 @@
         at = pl.multiple_of(k * 128, 128)
         before = pl.multiple_of(lax.rem(k + 7, 8) * 128, 128)
         after = pl.multiple_of(lax.rem(k + 1, 8) * 128, 128)
-        groups = factor([diag_ref[8 * g : 8 * g + 8, :] for g in range(16)])
-        inv = split3(jnp.where(lane <= sub, jnp.concatenate(groups, axis=0), 0.0))
+        top = factor([diag_ref[8 * g : 8 * g + 8, :] for g in range(8)], 0)
+        cross = split3(jnp.transpose(top, (1, 0))[64:, :])
+        known = split3(jnp.where((half_lane <= half_sub) | (half_lane >= 64), top, 0.0))
+        bottom = jnp.where(half_lane >= 64, diag_ref[64:, :], 0.0) - dot6(cross, known)
+        bottom = factor([bottom[8 * g : 8 * g + 8, :] for g in range(8)], 8)
+        halves = [
+            split3(jnp.where(half_lane <= half_sub + 64 * n, rows, 0.0)) for n, rows in enumerate((top, bottom))
+        ]
         x = settle(before)
         for n, part in enumerate(split3(jnp.transpose(x, (1, 0)))):
             for g in range(8):
@@ -158,10 +170,12 @@
             ls_ref[lax.rem(k + 1, 8), :, :depth], tuple(ref[:depth, pl.ds(after, 128)] for ref in xs_refs)
         )
         side_t = split3(jnp.transpose(row_ref[:, pl.ds(after, 128)], (1, 0)))
-        for ref, part in zip(ds_refs, inv):
-            ref[...] = part
-        xt = split3(dot6(side_t, inv, ((1,), (1,))))
-        diag_ref[...] = ahead - dot6(xt, xt, ((1,), (1,)))
+        for n, half in enumerate(halves):
+            for ref, part in zip(ds_refs, half):
+                ref[64 * n : 64 * n + 64, :] = part
+            xt = split3(dot6(side_t, half, ((1,), (1,))))
+            ahead = ahead - dot6(xt, xt, ((1,), (1,)))
+        diag_ref[...] = ahead
         return 0
 
     lax.fori_loop(0, 5, functools.partial(step, 512), 0)
@@ -202,13 +216,20 @@
 
 def panel_kernel(
     place_ref, row_ref, col_ref, high_ref, mid_ref, near0_ref, near1_ref, near2_ref, near3_ref, far_ref,
-    pr_ref, pc_ref, out_ref, p_ref, near_ref,
+    pr_ref, pc_ref, out_ref, rows_ref, cols_ref, near_ref, minus_ref, inverse_ref, sems,
 ):
     lane = lax.broadcasted_iota(jnp.int32, (256, 256), 1)
     step = pl.program_id(0)
 
     @pl.when(step == 0)
     def _():
+        copies = [
+            pltpu.make_async_copy(ref.at[pl.ds(256 * i, 256), :], inverse_ref.at[i, n], sems.at[i, n])
+            for i in range(4)
+            for n, ref in enumerate((high_ref, mid_ref))
+        ]
+        for copy in copies:
+            copy.start()
         for s, ref in enumerate((near0_ref, near1_ref, near2_ref, near3_ref)):
             source = lax.rem(place_ref[2] + 4 - s, 4)
             for q in range(2):
@@ -220,7 +241,9 @@
         for i in range(4):
             depth = 256 * (i + 1)
             rows = slice(256 * i, depth)
-            high, mid = high_ref[rows, :depth], mid_ref[rows, :depth]
+            copies[2 * i].wait()
+            copies[2 * i + 1].wait()
+            inverse = inverse_ref[i, :, :, :depth].reshape(512, depth)
             for t in range(6):
                 if t < 2:
                     right = near_ref[t, :depth, :]
@@ -228,18 +251,26 @@
                 else:
                     right = far_ref[: depth // 32, t - 2].reshape(depth, 256)
                     live = RSTEP * col_ref[t - 2]
-                solved = jnp.dot(high, right, preferred_element_type=F32)
-                solved = solved + jnp.dot(mid, right, preferred_element_type=F32)
-                p_ref[t, rows, :] = jnp.where(lane < live, solved, 0.0).astype(BF16)
+                solved = jnp.dot(inverse, right, preferred_element_type=F32)
+                solved = jnp.where(lane < live, solved[:256] + solved[256:], 0.0).astype(BF16)
+                if t < 2:
+                    rows_ref[t, rows, :] = solved
+                else:
+                    cols_ref[rows, 256 * t - 512 : 256 * t - 256] = solved
+        mine = pl.ds(pl.multiple_of(place_ref[0] * 128, 128), 128)
         for t in range(2):
-            pr_ref[t] = p_ref[t, pl.ds(pl.multiple_of(place_ref[0] * 128, 128), 128), :]
+            pr_ref[t] = rows_ref[t, mine, :]
+        mine = pl.ds(pl.multiple_of(place_ref[1] * 32, 32), 32)
         for t in range(4):
-            pc_ref[t] = p_ref[2 + t, pl.ds(pl.multiple_of(place_ref[1] * 32, 32), 32), :]
-
-    i, j = step // 4, lax.rem(step, 4)
-    coupling = lax.dot_general(p_ref[i], p_ref[2 + j], (((0,), (0,)), ((), ())), preferred_element_type=F32)
-    minus = (-coupling).astype(BF16)
-    out_ref[0, 0] = jnp.dot(near_ref[2 + i], minus, preferred_element_type=F32).astype(BF16)
+            pc_ref[t] = cols_ref[mine, 256 * t : 256 * t + 256]
+        for i in range(2):
+            coupling = lax.dot_general(
+                rows_ref[i], cols_ref[...], (((0,), (0,)), ((), ())), preferred_element_type=F32
+            )
+            for t in range(4):
+                minus_ref[4 * i + t] = (-coupling[:, 256 * t : 256 * t + 256]).astype(BF16)
+
+    out_ref[0, 0] = jnp.dot(near_ref[2 + step // 4], minus_ref[step], preferred_element_type=F32).astype(BF16)
 
 
 def panels(place, bucket_row, bucket_col, high, mid, near, far):
@@ -254,13 +285,20 @@
             jax.ShapeDtypeStruct((4, 32, 256), BF16),
             jax.ShapeDtypeStruct((2, 4, 1024, 256), BF16),
         ],
-        in_specs=[smem, smem, smem, *[full(array.shape) for array in arrays]],
+        in_specs=[smem, smem, smem, *[pl.BlockSpec(memory_space=pl.ANY)] * 2, *[full(array.shape) for array in arrays[2:]]],
         out_specs=[
             full((2, 128, 256)),
             full((4, 32, 256)),
             pl.BlockSpec((1, 1, 1024, 256), lambda s: (s // 4, lax.rem(s, 4), 0, 0)),
         ],
-        scratch_shapes=[pltpu.VMEM((6, 1024, 256), BF16), pltpu.VMEM((4, 1024, 256), BF16)],
+        scratch_shapes=[
+            pltpu.VMEM((2, 1024, 256), BF16),
+            pltpu.VMEM((1024, 1024), BF16),
+            pltpu.VMEM((4, 1024, 256), BF16),
+            pltpu.VMEM((8, 256, 256), BF16),
+            pltpu.VMEM((4, 2, 256, 1024), BF16),
+            pltpu.SemaphoreType.DMA((4, 2)),
+        ],
         compiler_params=pltpu.CompilerParams(vmem_limit_bytes=66_000_000),
         cost_estimate=pl.CostEstimate(flops=7 * 10**9, bytes_accessed=12 * 2**20, transcendentals=0),
         name="panels",
@@ -272,9 +310,16 @@
     return lax.ppermute(array, axis, [(k, (k + by) % count) for k in range(count)])
 
 
+def copies_for(array, axis):
+    return jnp.broadcast_to(array, (lax.axis_size(axis), *array.shape))
+
+
+def exchanged(copies, axis):
+    return lax.all_to_all(copies, axis, split_axis=0, concat_axis=0, tiled=True)
+
+
 def sent_to_all(array, axis):
-    copies = jnp.broadcast_to(array, (lax.axis_size(axis), *array.shape))
-    return lax.all_to_all(copies, axis, split_axis=0, concat_axis=0, tiled=True)
+    return exchanged(copies_for(array, axis), axis)
 
 
 def per_device(diag_tile, left_row, right_row, right_col, bucket_row, bucket_col):
@@ -289,9 +334,9 @@
     part = sent_to_all(part, ("y", "x"))
     near = jnp.stack([near, swapped])
     other = moved(part, "c", 1)
-    far = right_col.transpose(1, 0, 2)
+    far = copies_for(right_col.transpose(1, 0, 2), ROW)
     part, other, near, far = lax.optimization_barrier((part, other, near, far))
-    far = sent_to_all(far, ROW)
+    far = exchanged(far, ROW)
     near = [near, *[moved(near, "x", by) for by in range(1, 4)]]
     high, mid = chol_inverse(core[None], part, other)
     place = jnp.stack([lax.axis_index(COL), lax.axis_index(ROW), lax.axis_index("x"), lax.axis_index("zh")])

time: 138 us -> 136 us (0.986)
  Pallas kernels: 56.6 us -> 52.1 us
  waiting for transfers between devices: 21.5 us -> 24.3 us
    all_to_all x1, waiting for transfers between devices: 4.95 us -> 7.8 us  [exchanged(): return lax.all_to_all(copies, axis, split_axis=0, concat_axis=0, tiled=True)]
    pallas_call x1, Pallas kernels: 40.8 us -> 38 us  [chol_inverse(): pl.pallas_call(chol_kernel, out_shape=[jax.ShapeDtypeStruct((n, n), BF16)...]
    pallas_call x1, Pallas kernels: 15.8 us -> 14.1 us  [panels(): pl.pallas_call(panel_kernel, grid=(8,), out_shape=[jax.ShapeDtypeStruct((...]
    unnamed x14 -> x12, local copies, waits for them, and re-layouts: 5.47 us -> 4.3 us
  transfers between devices with their start and end apart: 6 -> 6, of which waited for: 2 -> 2; matrix products, arithmetic and copies ran while one was open for 1% -> 1% of each run, Pallas kernels for 30% -> 28%
where the time goes in v3:
time: 136 us; the launch traced here: 135 us
  Pallas kernels  52.1 us (38%)
  blocking collectives  38.6 us (28%)
  waiting for transfers between devices  24.3 us (18%)
  starting transfers between devices  11.3 us (8%)
  local copies, waits for them, and re-layouts  6.17 us (5%)
  other arithmetic  1.43 us (1%)
    all_to_all x2, blocking collectives, exchanged(): return lax.all_to_all(copies, axis, split_axis=0, concat_axis=0, tiled=True)  38.6 us
    pallas_call x1, Pallas kernels, chol_inverse(): pl.pallas_call(chol_kernel, out_shape=[jax.ShapeDtypeStruct((n, n), BF16)...  38 us
    ppermute x5, waiting for transfers between devices, moved(): lax.ppermute(array, axis, [(k, (k + by) % count) for k in range(count)])  16.5 us
    pallas_call x1, Pallas kernels, panels(): pl.pallas_call(panel_kernel, grid=(8,), out_shape=[jax.ShapeDtypeStruct((...  14.1 us
    all_to_all x1, waiting for transfers between devices, exchanged(): return lax.all_to_all(copies, axis, split_axis=0, concat_axis=0, tiled=True)  7.8 us
    ppermute x5, starting transfers between devices, moved(): lax.ppermute(array, axis, [(k, (k + by) % count) for k in range(count)])  6.75 us
    all_to_all x1, starting transfers between devices, exchanged(): return lax.all_to_all(copies, axis, split_axis=0, concat_axis=0, tiled=True)  4.55 us
    unnamed x12, local copies, waits for them, and re-layouts  4.3 us
  transfers between devices with their start and end apart: 6, of which 2 were waited for; matrix products, arithmetic and copies ran while one was open for 1% of the time, Pallas kernels for 28%

profile of v3, /device:TPU:33, one launch (start us, length us, event | category | flops | bytes accessed | tf_op | source)
XLA Modules:
  0.0 134.8 jit_solution(9378363802516571346)
XLA Ops:
  0.7 0.7 fusion.2
  1.4 0.0 copy-start.2
  1.4 0.0 copy-start.3
  1.4 14.1 %all_to_all.15 = f32[8,4,640]{2,1,0:T(4,128)S(1)} all-to-all(f32[8,4,640]{2,1,0:T(4,128)S(1)} %broadcast_in_dim.13), channel_id=1, replica_groups=mesh['zl'=4,'y'=4,'c'=2,'x'=4,'zh'=2] {'zl','zh'}, dimensions={0} | all-to-all | bytes 163840 | tf_op jit(solution)/shard_map/all_to_all | solution.py:318
  15.5 0.2 broadcast_in_dim.14
  15.7 0.0 copy-start.4
  15.7 24.6 %all_to_all.16.mine_ref = f32[16,8,4,640]{3,2,1,0:T(4,128)S(1)} all-to-all(f32[16,8,4,640]{3,2,1,0:T(4,128)S(1)} %broadcast_in_dim.14), channel_id=1, replica_groups=mesh['zl'=4,'y'=4,'c'=2,'x'=4,'zh'=2] {'y','x'}, dimensions={0} | all-to-all | bytes 2621440 | tf_op jit(solution)/shard_map/all_to_all | solution.py:318
  40.3 0.0 copy-start
  40.3 1.1 copy-done
  41.4 3.5 %collective-permute-start = (f32[16,8,4,640]{3,2,1,0:T(4,128)S(1)}, f32[16,8,4,640]{3,2,1,0:T(4,128)}, u32[]{:S(2)}, u32[]{:S(2)}) collective-permute-start(f32[16,8,4,640]{3,2,1,0:T(4,128)S(1)} %all_to_all.16.mine_ref), channel_id=1, source_target_pairs={{0,8},{8,0},{1,9},{9,1},{2,10},{10,2},{3,11},{11,3},{4,12},{12,4},... | collective-permute-start | bytes 3932168 | tf_op jit(solution)/shard_map/ppermute | solution.py:310
  44.9 0.0 copy-done.2
  44.9 0.0 copy-done.3
  45.0 1.3 collective-permute-start.1
  46.2 0.0 copy-done.4
  46.3 16.5 %collective-permute-done.1 = bf16[2,2,128,256]{3,2,1,0:T(8,128)(2,1)S(1)} collective-permute-done((bf16[2,2,128,256]{3,2,1,0:T(8,128)(2,1)S(1)}, bf16[2,2,128,256]{3,2,1,0:T(8,128)(2,1)S(1)}, u32[]{:S(2)}, u32[]{:S(2)}) %collective-permute-start.1) | collective-permute-done | bytes 262176 | tf_op jit(solution)/shard_map/ppermute | solution.py:310
  62.7 0.1 pad_maximum_fusion.near0_ref
  62.8 0.0 copy-start.1
  62.8 0.0 collective-permute-done.other_ref
  62.8 1.6 %broadcast_in_dim.15 = bf16[32,4,32,256]{3,2,1,0:T(8,128)(2,1)} broadcast(bf16[4,32,256]{2,1,0:T(8,128)(2,1)S(1)} %copy.11), dimensions={1,2,3} | broadcast | bytes 2162688 | tf_op jit(solution)/shard_map/broadcast_in_dim | solution.py:314
  64.4 4.6 %all-to-all-start.2 = ((bf16[32,4,32,256]{3,2,1,0:T(8,128)(2,1)}), bf16[32,4,32,256]{3,2,1,0:T(8,128)(2,1)}, u32[]{:S(2)}, u32[]{:S(2)}) async-start(bf16[32,4,32,256]{3,2,1,0:T(8,128)(2,1)} %broadcast_in_dim.15), calls=%async_computation.2 | async-start | bytes 4194304 | tf_op jit(solution)/shard_map/all_to_all | solution.py:318
  69.0 0.6 pad_add_fusion.place_ref
  69.6 0.5 collective-permute-start.4
  70.1 1.5 %collective-permute-start.3 = (bf16[2,2,2,128,256]{4,3,2,1,0:T(8,128)(2,1)S(1)}, bf16[2,2,2,128,256]{4,3,2,1,0:T(8,128)(2,1)}, u32[]{:S(2)}, u32[]{:S(2)}) collective-permute-start(bf16[2,2,2,128,256]{4,3,2,1,0:T(8,128)(2,1)S(1)} %pad_maximum_fusion.near0_ref), channel_id=1, source_target_pairs={{0,4},{2,6},{4,0},{6,2},{1,5},{3,7},{5,1},{7,3},{8,12},{10,14},{12... | collective-permute-start | bytes 1572872 | tf_op jit(solution)/shard_map/ppermute | solution.py:310
  71.6 0.0 copy-done.1
  71.6 0.0 collective-permute-start.2
  71.6 38.0 %chol_inverse.1 = (bf16[1024,1024]{1,0:T(8,128)(2,1)}, bf16[1024,1024]{1,0:T(8,128)(2,1)}) custom-call(s32[1]{0:T(128)} %bitcast.4.core_ref, f32[16,8,4,640]{3,2,1,0:T(4,128)} %copy-done, f32[16,8,4,640]{3,2,1,0:T(4,128)} %collective-permute-done.other_ref), custom_call_target="tpu_custom_call" | custom-call | flops 20000000000 | bytes 8388608 | tf_op jit(solution)/shard_map/chol_inverse/pallas_call | solution.py:197
  109.6 0.0 collective-permute-done.4.near3_ref
  109.6 0.0 collective-permute-done.3.near2_ref
  109.6 0.0 collective-permute-done.2.near1_ref
  109.6 7.8 %all-to-all-done.2.far_ref = bf16[32,4,32,256]{3,2,1,0:T(8,128)(2,1)} async-done(((bf16[32,4,32,256]{3,2,1,0:T(8,128)(2,1)}), bf16[32,4,32,256]{3,2,1,0:T(8,128)(2,1)}, u32[]{:S(2)}, u32[]{:S(2)}) %all-to-all-start.2) | async-done | bytes 2097184 | tf_op jit(solution)/shard_map/all_to_all | solution.py:318
  117.5 14.1 %panels.1 = (bf16[2,128,256]{2,1,0:T(8,128)(2,1)}, bf16[4,32,256]{2,1,0:T(8,128)(2,1)}, bf16[2,4,1024,256]{3,2,1,0:T(8,128)(2,1)}) custom-call(s32[4]{0:T(128)} %pad_add_fusion.place_ref, s32[2]{0:T(128)} %row_ref.1, s32[4]{0:T(128)} %col_ref.1, bf16[1024,1024]{1,0:T(8,128)(2,1)} %get-tuple-element.14.high_ref, ...), custom_call_target="tpu_custom_call" | custom-call | flops 7000000000 | bytes 12582912 | tf_op jit(solution)/shard_map/panels/pallas_call | solution.py:280
  131.6 1.7 %copy.12 = bf16[128,2,256]{2,1,0:T(2,128)(2,1)} copy(bf16[128,2,256]{2,0,1:T(8,128)(2,1)} %bitcast.19) | data formatting | bytes 262144
  133.3 1.5 %copy.13 = bf16[32,4,256]{2,1,0:T(4,128)(2,1)} copy(bf16[32,4,256]{2,0,1:T(8,128)(2,1)} %bitcast.21) | data formatting | bytes 131072
  (4 shorter events, 0.1 us)
Async XLA Ops:
  1.4 43.5 %copy-start.2 = (bf16[128,2,256]{2,1,0:T(2,128)(2,1)S(1)}, bf16[128,2,256]{2,1,0:T(2,128)(2,1)}, u32[]{:S(2)}) copy-start(bf16[128,2,256]{2,1,0:T(2,128)(2,1)} %param.7) | copy-start | bytes 393220
  1.4 43.5 %copy-start.3 = (bf16[128,2,256]{2,1,0:T(2,128)(2,1)S(1)}, bf16[128,2,256]{2,1,0:T(2,128)(2,1)}, u32[]{:S(2)}) copy-start(bf16[128,2,256]{2,1,0:T(2,128)(2,1)} %param.8) | copy-start | bytes 393220
  15.7 30.5 %copy-start.4 = (bf16[32,4,256]{2,1,0:T(4,128)(2,1)S(1)}, bf16[32,4,256]{2,1,0:T(4,128)(2,1)}, u32[]{:S(2)}) copy-start(bf16[32,4,256]{2,1,0:T(4,128)(2,1)} %param.9) | copy-start | bytes 196612
  40.3 1.1 copy-start
  41.4 21.4 %collective-permute-start = (f32[16,8,4,640]{3,2,1,0:T(4,128)S(1)}, f32[16,8,4,640]{3,2,1,0:T(4,128)}, u32[]{:S(2)}, u32[]{:S(2)}) collective-permute-start(f32[16,8,4,640]{3,2,1,0:T(4,128)S(1)} %all_to_all.16.mine_ref), channel_id=1, source_target_pairs={{0,8},{8,0},{1,9},{9,1},{2,10},{10,2},{3,11},{11,3},{4,12},{12,4},... | collective-permute-start | bytes 3932168 | tf_op jit(solution)/shard_map/ppermute | solution.py:310
  45.0 17.8 %collective-permute-start.1 = (bf16[2,2,128,256]{3,2,1,0:T(8,128)(2,1)S(1)}, bf16[2,2,128,256]{3,2,1,0:T(8,128)(2,1)S(1)}, u32[]{:S(2)}, u32[]{:S(2)}) collective-permute-start(bf16[2,2,128,256]{3,2,1,0:T(8,128)(2,1)S(1)} %get-tuple-element.25), channel_id=1, source_target_pairs={{0,1},{1,0},{2,3},{3,2},{4,5},{5,4},{6,7},{7,6},{8,9},{9,8},{10,11... | collective-permute-start | bytes 786440 | tf_op jit(solution)/shard_map/ppermute | solution.py:310
  62.8 8.8 %copy-start.1 = (bf16[2,2,2,128,256]{4,3,2,1,0:T(8,128)(2,1)}, bf16[2,2,2,128,256]{4,3,2,1,0:T(8,128)(2,1)S(1)}, u32[]{:S(2)}) copy-start(bf16[2,2,2,128,256]{4,3,2,1,0:T(8,128)(2,1)S(1)} %pad_maximum_fusion.near0_ref) | copy-start | bytes 1572868
  64.4 53.0 %all-to-all-start.2 = ((bf16[32,4,32,256]{3,2,1,0:T(8,128)(2,1)}), bf16[32,4,32,256]{3,2,1,0:T(8,128)(2,1)}, u32[]{:S(2)}, u32[]{:S(2)}) async-start(bf16[32,4,32,256]{3,2,1,0:T(8,128)(2,1)} %broadcast_in_dim.15), calls=%async_computation.2 | async-start | bytes 4194304 | tf_op jit(solution)/shard_map/all_to_all | solution.py:318
  69.6 40.0 %collective-permute-start.4 = (bf16[2,2,2,128,256]{4,3,2,1,0:T(8,128)(2,1)S(1)}, bf16[2,2,2,128,256]{4,3,2,1,0:T(8,128)(2,1)}, u32[]{:S(2)}, u32[]{:S(2)}) collective-permute-start(bf16[2,2,2,128,256]{4,3,2,1,0:T(8,128)(2,1)S(1)} %pad_maximum_fusion.near0_ref), channel_id=1, source_target_pairs={{0,6},{2,0},{4,2},{6,4},{1,7},{3,1},{5,3},{7,5},{8,14},{10,8},{12,... | collective-permute-start | bytes 1572872 | tf_op jit(solution)/shard_map/ppermute | solution.py:310
  70.1 39.6 %collective-permute-start.3 = (bf16[2,2,2,128,256]{4,3,2,1,0:T(8,128)(2,1)S(1)}, bf16[2,2,2,128,256]{4,3,2,1,0:T(8,128)(2,1)}, u32[]{:S(2)}, u32[]{:S(2)}) collective-permute-start(bf16[2,2,2,128,256]{4,3,2,1,0:T(8,128)(2,1)S(1)} %pad_maximum_fusion.near0_ref), channel_id=1, source_target_pairs={{0,4},{2,6},{4,0},{6,2},{1,5},{3,7},{5,1},{7,3},{8,12},{10,14},{12... | collective-permute-start | bytes 1572872 | tf_op jit(solution)/shard_map/ppermute | solution.py:310
  71.6 38.1 %collective-permute-start.2 = (bf16[2,2,2,128,256]{4,3,2,1,0:T(8,128)(2,1)S(1)}, bf16[2,2,2,128,256]{4,3,2,1,0:T(8,128)(2,1)}, u32[]{:S(2)}, u32[]{:S(2)}) collective-permute-start(bf16[2,2,2,128,256]{4,3,2,1,0:T(8,128)(2,1)S(1)} %pad_maximum_fusion.near0_ref), channel_id=1, source_target_pairs={{0,2},{2,4},{4,6},{6,0},{1,3},{3,5},{5,7},{7,1},{8,10},{10,12},{12... | collective-permute-start | bytes 1572872 | tf_op jit(solution)/shard_map/ppermute | solution.py:310
